TPU v7x, 128 devices: a whole 4x4x4 slice. The times are simulated.
128 devices in a mesh: data: 1, cp: 128 (over z, y, x, core).
Axes of the slice: x: 4, y: 4, z: 4, core: 2. Of those that a mesh axis runs over, the one named last changes fastest.
Arguments:
- q: bfloat16 [65536, 1, 128], P(('data', 'cp'))
- k: bfloat16 [65536, 1, 128], P(('data', 'cp'))
- v: bfloat16 [65536, 1, 128], P(('data', 'cp'))
- o: bfloat16 [65536, 1, 128], P(('data', 'cp'))
- dout: bfloat16 [65536, 1, 128], P(('data', 'cp'))
- lse: float32 [1, 65536], P(None, ('data', 'cp'))
Outputs:
- output 1: bfloat16 [65536, 1, 128], P(('data', 'cp'))
- output 2: bfloat16 [65536, 1, 128], P(('data', 'cp'))
- output 3: bfloat16 [65536, 1, 128], P(('data', 'cp'))
All inputs are finite; a program needn't handle non-finite values.
Results may differ from a plain program's by a relative error of at most 0.00164.
Values are sent between devices in bfloat16 or wider.
A program may use at most 1 GiB of HBM per device.

v0:
```python
import functools
import math

import jax
import jax.numpy as jnp
from jax import lax
from jax.experimental import pallas as pl
from jax.experimental.pallas import tpu as pltpu
from jax.sharding import PartitionSpec as P

F32, BF16 = jnp.float32, jnp.bfloat16
MESH = pl.DeviceIdType.MESH
ROWS, HD = 512, 128
L = 32
NC = ROWS // L
NG, GR = 8, 64
NQ, NK = 16, 8
BQ, BK = NQ * L, NK * L
KQ, KR = 4, 128
SCALE = HD ** -0.5
LOG2E = math.log2(math.e)


def dg(a, b, ca, cb):
    return lax.dot_general(a, b, (((ca,), (cb,)), ((), ())), preferred_element_type=F32)


def kernel(q_ref, k_ref, v_ref, o_ref, do_ref, lse_ref, dq_ref, dk_ref, dv_ref,
           qd, kv, ld, lb, db, thr, kt, vt, qt, dot, p_a, p_b, p_c, ds_a, ds_b, ds_c, dqt, dkt, dvt,
           pq, rb, sa, ra, pk, rd, sz, rz,
           lda_s, lda_r, ldb_s, ldb_r, qa_s, qa_r, qb_s, qb_r, kz_s, kz_r, kd_s, kd_r,
           rb_s, rb_r, ra_s, ra_r, rd_s, rd_r, rz_s, rz_r):
    me = lax.axis_index('cp')
    core = lax.rem(me, 2)
    x = lax.rem(lax.div(me, 2), 4)
    y = lax.rem(lax.div(me, 8), 4)
    z = lax.div(me, 32)
    a = x + core * (y - x)
    b = y + core * (x - y)
    step_a, step_b = 2 + 6 * core, 8 - 6 * core

    def dev_q(b_, a_):
        return z * 32 + b_ * step_b + a_ * step_a + core

    def dev_k(z_, c_):
        return z_ * 32 + y * 8 + x * 2 + c_

    def turn(i, d):
        return lax.rem(i + d, 4)

    def remote(src, dst, ss, rs, dev):
        return pltpu.make_async_remote_copy(src_ref=src, dst_ref=dst, send_sem=ss, recv_sem=rs,
                                            device_id={'cp': dev}, device_id_type=MESH)

    D3 = (1, 2, 3)
    slot = b * 4 + a

    def ld_a(d):
        return remote(ld.at[slot], ld.at[slot], lda_s.at[d - 1], lda_r.at[d - 1], dev_q(b, turn(a, d)))

    def ld_b(d):
        r = ld.at[pl.ds(b * 4, 4)]
        return remote(r, r, ldb_s.at[d - 1], ldb_r.at[d - 1], dev_q(turn(b, d), a))

    def q_a(g, d):
        r = qd.at[slot, :, pl.ds(pl.multiple_of(g * GR, GR), GR), :]
        return remote(r, r, qa_s.at[g, d - 1], qa_r.at[g, d - 1], dev_q(b, turn(a, d)))

    def q_b(g, d):
        r = qd.at[pl.ds(b * 4, 4), :, pl.ds(pl.multiple_of(g * GR, GR), GR), :]
        return remote(r, r, qb_s.at[g, d - 1], qb_r.at[g, d - 1], dev_q(turn(b, d), a))

    def k_z(j, d):
        r = kv.at[core, z, :, pl.ds(pl.multiple_of(j * KR, KR), KR), :]
        return remote(r, r, kz_s.at[j, d - 1], kz_r.at[j, d - 1], dev_k(turn(z, d), core))

    def k_d(j, d):
        r = kv.at[core, turn(z, 4 - d), :, pl.ds(pl.multiple_of(j * KR, KR), KR), :]
        return remote(r, r, kd_s.at[j, d], kd_r.at[j, d], dev_k(z, 1 - core))

    def r_b(g, d):
        return remote(pq.at[g, pl.ds(turn(b, d) * 4, 4)], rb.at[g, d - 1], rb_s.at[g, d - 1], rb_r.at[g, d - 1],
                      dev_q(turn(b, d), a))

    def r_a(g, d):
        return remote(sa.at[g, turn(a, d)], ra.at[g, d - 1], ra_s.at[g, d - 1], ra_r.at[g, d - 1],
                      dev_q(b, turn(a, d)))

    def r_d(g):
        return remote(pk.at[g, 1 - core], rd.at[g], rd_s.at[g], rd_r.at[g], dev_k(z, 1 - core))

    def r_z(g, d):
        return remote(sz.at[g, turn(z, d)], rz.at[g, d - 1], rz_s.at[g, d - 1], rz_r.at[g, d - 1],
                      dev_k(turn(z, d), core))

    qd[slot, 0] = q_ref[...]
    qd[slot, 1] = do_ref[...]
    kv[core, z, 0] = k_ref[...]
    kv[core, z, 1] = v_ref[...]
    for j in range(4):
        rows_j = pl.ds(j * 128, 128)
        d_j = jnp.sum(do_ref[rows_j, :].astype(F32) * o_ref[rows_j, :].astype(F32), axis=1, keepdims=True)
        ld[slot, pl.ds(j, 1), :] = lse_ref[:, rows_j] * LOG2E
        ld[slot, pl.ds(4 + j, 1), :] = jnp.broadcast_to(d_j, (128, 128)).T[:1]

    barrier = pltpu.get_barrier_semaphore()
    peers = [dev_q(b, turn(a, d)) for d in D3] + [dev_q(turn(b, d), a) for d in D3]
    peers += [dev_k(turn(z, d), core) for d in D3] + [dev_k(z, 1 - core)]
    for p in peers:
        pl.semaphore_signal(barrier, inc=1, device_id={'cp': p}, device_id_type=MESH)
    pl.semaphore_wait(barrier, len(peers))

    for d in D3:
        ld_a(d).start()
    for d in D3:
        q_a(NG - 1, d).start()
    for j in range(KQ):
        for d in D3:
            k_z(j, d).start()
        k_d(j, 0).start()

    def start_a(i, _):
        for d in D3:
            q_a(NG - 2 - i, d).start()
        return 0
    lax.fori_loop(0, NG - 1, start_a, 0)

    for d in D3:
        ld_a(d).wait_recv()
    for d in D3:
        ld_b(d).start()

    qi = lax.broadcasted_iota(jnp.int32, (BQ, 1), 0)
    ki = lax.broadcasted_iota(jnp.int32, (1, BK), 1)
    qpos = (qi & (L - 1)) * 128 + dev_q(qi >> 7, (qi >> 5) & 3)
    kpos = (ki & (L - 1)) * 128 + dev_k((ki >> 5) & 3, ki >> 7)
    thr[0] = jnp.full((BQ, BK), jnp.inf, F32)
    thr[1] = jnp.where(kpos <= qpos, jnp.inf, -jnp.inf).astype(F32)
    dkt[...] = jnp.zeros_like(dkt)
    dvt[...] = jnp.zeros_like(dvt)
    dqt[...] = jnp.zeros_like(dqt)

    def pass_a(i, _):
        g = NG - 1 - i
        for d in D3:
            q_a(g, d).wait_recv()
        for d in D3:
            q_b(g, d).start()
        return 0
    lax.fori_loop(0, 2, pass_a, 0)

    for d in D3:
        ld_b(d).wait_recv()

    def prep_l(i, _):
        for j in range(4):
            rows_j = pl.ds(j * 128, 128)
            lb[i, rows_j, :] = jnp.broadcast_to(ld[i, pl.ds(j, 1), :], (128, 128)).T
            db[i, rows_j, :] = jnp.broadcast_to(ld[i, pl.ds(4 + j, 1), :], (128, 128)).T
        return 0

    def pass_k(j, _):
        for d in D3:
            k_z(j, d).wait_recv()
        for d in D3:
            k_d(j, d).start()
        return 0
    lax.fori_loop(0, KQ, pass_k, 0)
    lax.fori_loop(0, NQ, prep_l, 0)
    lax.fori_loop(2, NG, pass_a, 0)

    def rows_q(which, r):
        return qd[:, which, pl.ds(pl.multiple_of(r * L, L), L), :].reshape(BQ, HD)

    def rows_k(which, c):
        return kv[:, :, which, pl.ds(pl.multiple_of(c * L, L), L), :].reshape(BK, HD)

    def rows_f(ref, r):
        return ref[:, pl.ds(pl.multiple_of(r * L, L), L), :].reshape(BQ, HD)

    def prep_k(c, _):
        kt[c] = rows_k(0, c).T
        vt[c] = rows_k(1, c).T
        return 0

    def take_k(j, _):
        for d in (0, 1, 2, 3):
            k_d(j, d).wait_recv()
        lax.fori_loop(j * (KR // L), (j + 1) * (KR // L), prep_k, 0)
        return 0
    lax.fori_loop(0, KQ, take_k, 0)

    def a_mm(r, c):
        return dg(rows_q(0, r), kt[c], 1, 0), dg(rows_q(1, r), vt[c], 1, 0)

    def a_vpu(r, sdp, diag, p_s, ds_s):
        s, dp = sdp
        lbr, dbr = rows_f(lb, r), rows_f(db, r)
        t = s * (SCALE * LOG2E) - jnp.concatenate([lbr, lbr], axis=1)
        p = jnp.exp2(jnp.minimum(t, thr[diag]))
        p_s[...] = p.astype(BF16)
        ds_s[...] = (p * (dp - jnp.concatenate([dbr, dbr], axis=1))).astype(BF16)

    def b_mm(c, h, p_s, ds_s):
        p, ds = p_s[...], ds_s[...]
        dqt[h] += dg(kt[c], ds, 1, 1)
        return dg(dot[h], p, 1, 0), dg(qt[h], ds, 1, 0)

    def q_prep(r, h):
        qt[h] = rows_q(0, r).T
        dot[h] = rows_q(1, r).T

    def finish_q(g, h):
        pq[g, :, pl.ds(h * L, L), :] = dqt[h].T.reshape(NQ, L, HD)
        dqt[h] = jnp.zeros((HD, BQ), F32)

    def finish_k(g, h):
        r = 2 * g + h
        pk[g, :, :, 0, pl.ds(h * L, L), :] = dkt[r].T.reshape(2, 4, L, HD)
        pk[g, :, :, 1, pl.ds(h * L, L), :] = dvt[r].T.reshape(2, 4, L, HD)

    def one(c, r0, d0):
        sdp = a_mm(r0, c + 1)
        dv, dk = b_mm(c, 0, p_a, ds_a)
        a_vpu(r0, sdp, d0, p_a, ds_a)
        sdp = a_mm(r0 + 1, c + 1)
        dv1, dk1 = b_mm(c, 1, p_b, ds_b)
        a_vpu(r0 + 1, sdp, 0, p_b, ds_b)
        dvt[c] += dv + dv1
        dkt[c] += dk + dk1

    def inner(r0):
        def two(j, _):
            c = 2 * j
            one(c, r0, 0)
            one(c + 1, r0, lax.div(c + 2, r0))
            return 0
        lax.fori_loop(0, lax.div(r0, 2), two, 0)

    def tail(g, nxt):
        r0, r1 = 2 * g, 2 * g + 1
        sdp = a_mm(r1, r1)
        dv, dk = b_mm(r0, 0, p_a, ds_a)
        a_vpu(r1, sdp, 1, p_c, ds_c)
        if nxt:
            sdp = a_mm(r0 - 2, 0)
        dv1, dk1 = b_mm(r0, 1, p_b, ds_b)
        if nxt:
            a_vpu(r0 - 2, sdp, lax.div(2, r0), p_a, ds_a)
        dvt[r0] += dv + dv1
        dkt[r0] += dk + dk1
        if nxt:
            sdp = a_mm(r0 - 1, 0)
        dv, dk = b_mm(r1, 1, p_c, ds_c)
        if nxt:
            a_vpu(r0 - 1, sdp, 0, p_b, ds_b)
        dvt[r1] += dv
        dkt[r1] += dk
        finish_q(g, 0)
        finish_k(g, 0)
        finish_q(g, 1)
        finish_k(g, 1)
        if nxt:
            q_prep(r0 - 2, 0)
            q_prep(r0 - 1, 1)

    def rs1(g):
        for d in D3:
            r_b(g, d).start()
        r_d(g).start()

    def rs2(g):
        r_d(g).wait_recv()
        sz[g] = pk[g, core] + rd[g]
        for d in D3:
            r_z(g, d).start()
        for d in D3:
            r_b(g, d).wait_recv()
        sa[g] = pq[g, pl.ds(b * 4, 4)] + rb[g, 0] + rb[g, 1] + rb[g, 2]
        for d in D3:
            r_a(g, d).start()

    def rs3(g):
        for d in D3:
            r_z(g, d).wait_recv()
        rows_g = pl.ds(pl.multiple_of(g * GR, GR), GR)
        dkv = sz[g, z] + rz[g, 0] + rz[g, 1] + rz[g, 2]
        dk_ref[rows_g, :] = (dkv[0] * SCALE).astype(BF16)
        dv_ref[rows_g, :] = dkv[1].astype(BF16)
        for d in D3:
            r_a(g, d).wait_recv()
        dq = sa[g, a] + ra[g, 0] + ra[g, 1] + ra[g, 2]
        dq_ref[rows_g, :] = (dq * SCALE).astype(BF16)

    def take_q(g):
        for d in D3:
            q_b(g, d).wait_recv()

    take_q(NG - 1)
    q_prep(NC - 2, 0)
    q_prep(NC - 1, 1)
    a_vpu(NC - 2, a_mm(NC - 2, 0), 0, p_a, ds_a)
    a_vpu(NC - 1, a_mm(NC - 1, 0), 0, p_b, ds_b)

    def superstep(i, _):
        g = NG - 1 - i
        inner(2 * g)
        take_q(g - 1)
        tail(g, True)
        rs1(g)

        @pl.when(i >= 1)
        def _():
            rs2(g + 1)

        @pl.when(i >= 2)
        def _():
            rs3(g + 2)
        return 0
    lax.fori_loop(0, NG - 1, superstep, 0)
    tail(0, False)
    rs1(0)
    rs2(1)
    rs3(2)
    rs2(0)
    rs3(1)
    rs3(0)

    for d in D3:
        ld_a(d).wait_send()
        ld_b(d).wait_send()

    def sent_k(j, _):
        for d in D3:
            k_z(j, d).wait_send()
        for d in (0, 1, 2, 3):
            k_d(j, d).wait_send()
        return 0
    lax.fori_loop(0, KQ, sent_k, 0)

    def sent(g, _):
        r_d(g).wait_send()
        for d in D3:
            for f in (q_a, q_b, r_b, r_a, r_z):
                f(g, d).wait_send()
        return 0
    lax.fori_loop(0, NG, sent, 0)


def local(q, k, v, o, dout, lse):
    flat = (ROWS, HD)
    vm = pl.BlockSpec(memory_space=pltpu.VMEM)
    V, DMA = pltpu.VMEM, pltpu.SemaphoreType.DMA
    scratch = [
        V((NQ, 2, ROWS, HD), BF16), V((2, 4, 2, ROWS, HD), BF16), V((NQ, 8, 128), F32),
        V((NQ, ROWS, HD), F32), V((NQ, ROWS, HD), F32), V((2, BQ, BK), F32),
        V((NC, HD, BK), BF16), V((NC, HD, BK), BF16), V((2, HD, BQ), BF16), V((2, HD, BQ), BF16),
        *[V((BQ, BK), BF16)] * 6,
        V((2, HD, BQ), F32), V((NC, HD, BK), F32), V((NC, HD, BK), F32),
        V((NG, NQ, GR, HD), F32), V((NG, 3, 4, GR, HD), F32), V((NG, 4, GR, HD), F32), V((NG, 3, GR, HD), F32),
        V((NG, 2, 4, 2, GR, HD), F32), V((NG, 4, 2, GR, HD), F32), V((NG, 4, 2, GR, HD), F32),
        V((NG, 3, 2, GR, HD), F32),
        *[DMA((3,))] * 4, *[DMA((NG, 3))] * 4, *[DMA((KQ, 3))] * 2, *[DMA((KQ, 4))] * 2,
        *[DMA((NG, 3))] * 4, *[DMA((NG,))] * 2, *[DMA((NG, 3))] * 2,
    ]
    outs = pl.pallas_call(
        kernel,
        out_shape=[jax.ShapeDtypeStruct(flat, BF16)] * 3,
        in_specs=[vm] * 6, out_specs=[vm] * 3,
        scratch_shapes=scratch,
        compiler_params=pltpu.CompilerParams(collective_id=0, has_side_effects=True, vmem_limit_bytes=62 << 20),
    )(*[t.reshape(flat) for t in (q, k, v, o, dout)], lse)
    return tuple(t.reshape(ROWS, 1, HD) for t in outs)


def solution(mesh):
    rows = P(('data', 'cp'))
    cols = P(None, ('data', 'cp'))
    return jax.shard_map(local, mesh=mesh, in_specs=(rows, rows, rows, rows, rows, cols),
                         out_specs=(rows, rows, rows), check_vma=False)
```

profile of v0, /device:TPU:0, one launch (start us, length us, event | category | flops | bytes accessed | tf_op | source)
XLA Modules:
  0.0 97.9 jit_solution(3239066703598916251)
XLA Ops:
  0.6 94.0 %shard_map.85 = (bf16[512,128]{1,0:T(8,128)(2,1)}, bf16[512,128]{1,0:T(8,128)(2,1)}, bf16[512,128]{1,0:T(8,128)(2,1)}) custom-call(bf16[512,128]{1,0:T(8,128)(2,1)} %bitcast.8, bf16[512,128]{1,0:T(8,128)(2,1)} %bitcast.9, bf16[512,128]{1,0:T(8,128)(2,1)} %bitcast.10, bf16[512,128]{1,0:T(8,128)(2,1)} %bitcast.11, bf16[512,128]{1,0:T(8,128)(2,1)} %bitcast.12, ...), custom_call_target="tpu_custom_call" | custom-call | tf_op jit(solution)/shard_map/pallas_call | solution.py:366
  94.7 0.0 copy-start.1
  94.7 1.6 %copy.12 = bf16[512,1,128]{2,0,1:T(8,128)(2,1)} copy(bf16[512,1,128]{2,0,1:T(8,128)(2,1)} %bitcast.15) | data formatting | bytes 262144
  96.3 0.0 copy-done.1
  96.3 0.0 copy-start
  96.3 0.7 copy.13
  97.0 0.3 copy-done
  97.2 0.7 copy.14
Async XLA Ops:
  94.7 1.6 %copy-start.1 = (bf16[512,128]{1,0:T(8,128)(2,1)S(1)}, bf16[512,128]{1,0:T(8,128)(2,1)}, u32[]{:S(2)}) copy-start(bf16[512,128]{1,0:T(8,128)(2,1)} %get-tuple-element.7) | copy-start | bytes 393220
  96.3 1.0 copy-start
where the time goes:
time: 98.1 us; the launch traced here: 97.9 us
  Pallas kernels  94 us (96%)
  local copies, waits for them, and re-layouts  3.21 us (3%)
    pallas_call x1, Pallas kernels, local(): pl.pallas_call(kernel, out_shape=[jax.ShapeDtypeStruct(flat, BF16)] * 3,...  94 us
    unnamed x7, local copies, waits for them, and re-layouts  3.21 us

commit v1 on v0

v1 whole, which is shorter than its diff:
```python
import functools
import math

import jax
import jax.numpy as jnp
from jax import lax
from jax.experimental import pallas as pl
from jax.experimental.pallas import tpu as pltpu
from jax.sharding import PartitionSpec as P

F32, BF16 = jnp.float32, jnp.bfloat16
MESH = pl.DeviceIdType.MESH
ROWS, HD = 512, 128
L = 32
NC = ROWS // L
NG, GR = 8, 64
NQ, NK = 16, 8
BQ, BK = NQ * L, NK * L
KQ, KR = 4, 128
SCALE = HD ** -0.5
LOG2E = math.log2(math.e)


def dg(a, b, ca, cb):
    return lax.dot_general(a, b, (((ca,), (cb,)), ((), ())), preferred_element_type=F32)


def kernel(q_hbm, k_hbm, v_hbm, o_hbm, do_hbm, lse_hbm, dq_ref, dk_ref, dv_ref,
           qd, kv, ld, ex, thr, kt, vt, qt, dot, p_a, p_b, p_c, ds_a, ds_b, ds_c, dqt, dkt, dvt,
           pq, rb, sa, ra, pk, rd, sz, rz, o_in, lse_in,
           in_s, lda_s, lda_r, ldb_s, ldb_r, qa_s, qa_r, qb_s, qb_r, kz_s, kz_r, kd_s, kd_r,
           rb_s, rb_r, ra_s, ra_r, rd_s, rd_r, rz_s, rz_r):
    me = lax.axis_index('cp')
    core = lax.rem(me, 2)
    x = lax.rem(lax.div(me, 2), 4)
    y = lax.rem(lax.div(me, 8), 4)
    z = lax.div(me, 32)
    a = x + core * (y - x)
    b = y + core * (x - y)
    step_a, step_b = 2 + 6 * core, 8 - 6 * core

    def dev_q(b_, a_):
        return z * 32 + b_ * step_b + a_ * step_a + core

    def dev_k(z_, c_):
        return z_ * 32 + y * 8 + x * 2 + c_

    def turn(i, d):
        return lax.rem(i + d, 4)

    def remote(src, dst, ss, rs, dev):
        return pltpu.make_async_remote_copy(src_ref=src, dst_ref=dst, send_sem=ss, recv_sem=rs,
                                            device_id={'cp': dev}, device_id_type=MESH)

    D3 = (1, 2, 3)
    slot = b * 4 + a

    def rows_g(g):
        return pl.ds(pl.multiple_of(g * GR, GR), GR)

    def ld_a(d):
        return remote(ld.at[slot], ld.at[slot], lda_s.at[d - 1], lda_r.at[d - 1], dev_q(b, turn(a, d)))

    def ld_b(d):
        r = ld.at[pl.ds(b * 4, 4)]
        return remote(r, r, ldb_s.at[d - 1], ldb_r.at[d - 1], dev_q(turn(b, d), a))

    def q_a(g, d):
        r = qd.at[slot, :, rows_g(g), :]
        return remote(r, r, qa_s.at[g, d - 1], qa_r.at[g, d - 1], dev_q(b, turn(a, d)))

    def q_b(g, d):
        r = qd.at[pl.ds(b * 4, 4), :, rows_g(g), :]
        return remote(r, r, qb_s.at[g, d - 1], qb_r.at[g, d - 1], dev_q(turn(b, d), a))

    def q_n(g, n):
        r = qd.at[pl.ds(b * 4, 4), :, rows_g(g), :]
        return remote(r, r, qb_s.at[g, n], qb_r.at[g, n], dev_q(turn(b, 1 + 2 * n), a))

    def q_f(g, n):
        r = qd.at[pl.ds(turn(b, 3 - 2 * n) * 4 + 2 * n, 2), :, rows_g(g), :]
        return remote(r, r, qb_s.at[g, 2 + n], qb_r.at[g, 2 + n], dev_q(turn(b, 1 + 2 * n), a))

    def k_z(j, d):
        r = kv.at[core, z, :, pl.ds(pl.multiple_of(j * KR, KR), KR), :]
        return remote(r, r, kz_s.at[j, d - 1], kz_r.at[j, d - 1], dev_k(turn(z, d), core))

    def k_d(j, d):
        r = kv.at[core, turn(z, 4 - d), :, pl.ds(pl.multiple_of(j * KR, KR), KR), :]
        return remote(r, r, kd_s.at[j, d], kd_r.at[j, d], dev_k(z, 1 - core))

    def r_b(g, d):
        return remote(pq.at[g, pl.ds(turn(b, d) * 4, 4)], rb.at[g, d - 1], rb_s.at[g, d - 1], rb_r.at[g, d - 1],
                      dev_q(turn(b, d), a))

    def r_a(g, d):
        return remote(sa.at[g, turn(a, d)], ra.at[g, d - 1], ra_s.at[g, d - 1], ra_r.at[g, d - 1],
                      dev_q(b, turn(a, d)))

    def r_d(g):
        return remote(pk.at[g, 1 - core], rd.at[g], rd_s.at[g], rd_r.at[g], dev_k(z, 1 - core))

    def r_z(g, d):
        return remote(sz.at[g, turn(z, d)], rz.at[g, d - 1], rz_s.at[g, d - 1], rz_r.at[g, d - 1],
                      dev_k(turn(z, d), core))

    barrier = pltpu.get_barrier_semaphore()
    peers = [dev_q(b, turn(a, d)) for d in D3] + [dev_q(turn(b, d), a) for d in D3]
    peers += [dev_k(turn(z, d), core) for d in D3] + [dev_k(z, 1 - core)]
    for p in peers:
        pl.semaphore_signal(barrier, inc=1, device_id={'cp': p}, device_id_type=MESH)
    ins = [(do_hbm, qd.at[slot, 1]), (o_hbm, o_in), (lse_hbm, lse_in), (q_hbm, qd.at[slot, 0]),
           (k_hbm, kv.at[core, z, 0]), (v_hbm, kv.at[core, z, 1])]
    ins = [pltpu.make_async_copy(src, dst, in_s.at[n]) for n, (src, dst) in enumerate(ins)]
    for c in ins:
        c.start()
    qi = lax.broadcasted_iota(jnp.int32, (BQ, 1), 0)
    ki = lax.broadcasted_iota(jnp.int32, (1, BK), 1)
    qpos = (qi & (L - 1)) * 128 + dev_q(qi >> 7, (qi >> 5) & 3)
    kpos = (ki & (L - 1)) * 128 + dev_k((ki >> 5) & 3, ki >> 7)
    thr[0] = jnp.full((BQ, BK), jnp.inf, F32)
    thr[1] = jnp.where(kpos <= qpos, jnp.inf, -jnp.inf).astype(F32)
    for c in ins:
        c.wait()
    def split(t):
        hi = t.astype(BF16).astype(F32)
        mid = (t - hi).astype(BF16).astype(F32)
        return hi, mid, t - hi - mid

    with jax.named_scope('own_ld'):
        ld[slot] = jnp.zeros((4, 8, 128), F32)
        for j in range(4):
            rows_j = pl.ds(j * 128, 128)
            d_j = jnp.sum(qd[slot, 1, rows_j, :].astype(F32) * o_in[rows_j, :].astype(F32), axis=1, keepdims=True)
            d_j = jnp.broadcast_to(d_j, (128, 128)).T[:1]
            for n, t in enumerate(split(lse_in[:, rows_j] * (-1.0 / SCALE)) + split(-d_j)):
                ld[slot, j, pl.ds(n, 1), :] = t
    with jax.named_scope('barrier'):
        pl.semaphore_wait(barrier, len(peers))

    def start_a(g):
        for d in D3:
            q_a(g, d).start()

    for d in D3:
        ld_a(d).start()
    for d in D3:
        k_z(0, d).start()
    k_d(0, 0).start()
    start_a(7)

    def start_k(j, _):
        for d in D3:
            k_z(j, d).start()
        k_d(j, 0).start()
        return 0
    lax.fori_loop(1, KQ, start_k, 0)
    ex[...] = jnp.zeros_like(ex)
    ri = lax.broadcasted_iota(jnp.int32, (HD, BK), 0)
    for c in range(NC):
        kt[c, HD:] = jnp.where(ri < 3, 1.0, 0.0).astype(BF16)
        vt[c, HD:] = jnp.where((ri >= 3) & (ri < 6), 1.0, 0.0).astype(BF16)
    dkt[...] = jnp.zeros_like(dkt)
    dvt[...] = jnp.zeros_like(dvt)
    dqt[...] = jnp.zeros_like(dqt)

    def got_a(g):
        for d in D3:
            q_a(g, d).wait_recv()

    def prep_e(i, _):
        for n in range(2):
            for j in range(4):
                ex[2 * i + n, pl.ds(j * 128, 128), pl.ds(0, 8)] = ld[2 * i + n, j].T.astype(BF16)
        return 0

    def pass_k(j):
        with jax.named_scope('pass_k'):
            for d in D3:
                k_z(j, d).wait_recv()
        for d in D3:
            k_d(j, d).start()

    with jax.named_scope('w_lda'):
        for d in D3:
            ld_a(d).wait_recv()
    for d in D3:
        ld_b(d).start()
    with jax.named_scope('got_a7'):
        got_a(7)
    for d in D3:
        q_b(7, d).start()
    start_a(6)
    start_a(5)
    pass_k(0)
    with jax.named_scope('w_ldb'):
        for d in D3:
            ld_b(d).wait_recv()
    with jax.named_scope('prep_e'):
        lax.fori_loop(0, NQ // 2, prep_e, 0)
    start_a(0)
    start_a(4)

    def rows_q(which, r):
        return qd[:, which, pl.ds(pl.multiple_of(r * L, L), L), :].reshape(BQ, HD)

    def rows_k(which, c):
        return kv[:, :, which, pl.ds(pl.multiple_of(c * L, L), L), :].reshape(BK, HD)

    def rows_e(r):
        return ex[:, pl.ds(pl.multiple_of(r * L, L), L), :].reshape(BQ, HD)

    def prep_k(c, _):
        kt[c, :HD] = rows_k(0, c).T
        vt[c, :HD] = rows_k(1, c).T
        return 0

    def take_k(j):
        with jax.named_scope('take_k'):
            for d in (0, 1, 2, 3):
                k_d(j, d).wait_recv()
        lax.fori_loop(j * (KR // L), (j + 1) * (KR // L), prep_k, 0)

    def a_mm(r, c):
        e = rows_e(r)
        return (dg(jnp.concatenate([rows_q(0, r), e], axis=1), kt[c], 1, 0),
                dg(jnp.concatenate([rows_q(1, r), e], axis=1), vt[c], 1, 0))

    def a_vpu(sdp, diag, p_s, ds_s):
        s, dp = sdp
        t = s * (SCALE * LOG2E)
        if diag is not None:
            t = jnp.minimum(t, thr[diag])
        p = jnp.exp2(t)
        p_s[...] = p.astype(BF16)
        ds_s[...] = (p * dp).astype(BF16)

    def b_mm(c, h, p_s, ds_s):
        p, ds = p_s[...], ds_s[...]
        dqt[h] += dg(kt[c, :HD], ds, 1, 1)
        return dg(dot[h], p, 1, 0), dg(qt[h], ds, 1, 0)

    def q_prep(r, h):
        qt[h] = rows_q(0, r).T
        dot[h] = rows_q(1, r).T

    def finish_q(g, h):
        pq[g, :, pl.ds(h * L, L), :] = dqt[h].T.reshape(NQ, L, HD)
        dqt[h] = jnp.zeros((HD, BQ), F32)

    def finish_k(g, h):
        r = 2 * g + h
        pk[g, :, :, 0, pl.ds(h * L, L), :] = dkt[r].T.reshape(2, 4, L, HD)
        pk[g, :, :, 1, pl.ds(h * L, L), :] = dvt[r].T.reshape(2, 4, L, HD)

    def one(c, r0, d0):
        sdp = a_mm(r0, c + 1)
        dv, dk = b_mm(c, 0, p_a, ds_a)
        a_vpu(sdp, d0, p_a, ds_a)
        sdp = a_mm(r0 + 1, c + 1)
        dv1, dk1 = b_mm(c, 1, p_b, ds_b)
        a_vpu(sdp, None, p_b, ds_b)
        dvt[c] += dv + dv1
        dkt[c] += dk + dk1

    def two(c, r0):
        one(c, r0, None)
        one(c + 1, r0, lax.div(c + 2, r0))

    def tail(g, nxt=None):
        r0, r1 = 2 * g, 2 * g + 1
        sdp = a_mm(r1, r1)
        dv, dk = b_mm(r0, 0, p_a, ds_a)
        a_vpu(sdp, 1, p_c, ds_c)
        if nxt is not None:
            sdp = a_mm(2 * nxt, 0)
        dv1, dk1 = b_mm(r0, 1, p_b, ds_b)
        if nxt is not None:
            a_vpu(sdp, lax.div(7 - nxt, 7), p_a, ds_a)
        dvt[r0] += dv + dv1
        dkt[r0] += dk + dk1
        if nxt is not None:
            sdp = a_mm(2 * nxt + 1, 0)
        dv, dk = b_mm(r1, 1, p_c, ds_c)
        if nxt is not None:
            a_vpu(sdp, None, p_b, ds_b)
        dvt[r1] += dv
        dkt[r1] += dk
        finish_q(g, 0)
        finish_k(g, 0)
        finish_q(g, 1)
        finish_k(g, 1)
        if nxt is not None:
            q_prep(2 * nxt, 0)
            q_prep(2 * nxt + 1, 1)

    def send_q(g):
        for d in D3:
            r_b(g, d).start()

    def send_k(g):
        r_d(g).start()

    def mid_q(g):
        with jax.named_scope('mid_q'):
            for d in D3:
                r_b(g, d).wait_recv()
            sa[g] = pq[g, pl.ds(b * 4, 4)] + rb[g, 0] + rb[g, 1] + rb[g, 2]
        for d in D3:
            r_a(g, d).start()

    def mid_k(g):
        with jax.named_scope('mid_k'):
            r_d(g).wait_recv()
            sz[g] = pk[g, core] + rd[g]
        for d in D3:
            r_z(g, d).start()

    def end_q(g):
        with jax.named_scope('end_q'):
            for d in D3:
                r_a(g, d).wait_recv()
            dq = sa[g, a] + ra[g, 0] + ra[g, 1] + ra[g, 2]
            dq_ref[rows_g(g), :] = (dq * SCALE).astype(BF16)

    def end_k(g):
        with jax.named_scope('end_k'):
            for d in D3:
                r_z(g, d).wait_recv()
            dkv = sz[g, z] + rz[g, 0] + rz[g, 1] + rz[g, 2]
            dk_ref[rows_g(g), :] = (dkv[0] * SCALE).astype(BF16)
            dv_ref[rows_g(g), :] = dkv[1].astype(BF16)

    def pass_q(g):
        with jax.named_scope('pass_q'):
            for n in (0, 1):
                q_n(g, n).wait_recv()
        for n in (0, 1):
            q_f(g, n).start()

    def next_q(g):
        with jax.named_scope('next_q'):
            got_a(g)
        for n in (0, 1):
            q_n(g, n).start()

    take_k(0)
    with jax.named_scope('first_q'):
        for d in D3:
            q_b(7, d).wait_recv()
    q_prep(14, 0)
    q_prep(15, 1)
    with jax.named_scope('first'):
        a_vpu(a_mm(14, 0), None, p_a, ds_a)
        a_vpu(a_mm(15, 0), None, p_b, ds_b)
    next_q(6)
    for g in (3, 2, 1):
        start_a(g)
    pass_k(1)

    def group(i):
        late = lax.div(i + 4, 8)
        return 7 - i + late - 4 * (lax.div(i + 5, 8) - late)

    def at(events, j):
        for when, act in events.items():
            pl.when(j == when)(act)

    def runs(*acts):
        def run():
            for f, arg in acts:
                f(arg)
        return run

    ahead = {
        0: {1: runs((take_k, 1), (next_q, 5)), 2: runs((pass_k, 2), (next_q, 0)), 3: runs((take_k, 2), (next_q, 4)),
            4: runs((pass_k, 3), (pass_q, 6), (next_q, 3)), 5: runs((take_k, 3), (pass_q, 5), (next_q, 2)),
            6: runs((pass_q, 0), (next_q, 1))},
        1: {1: runs((pass_q, 3)), 2: runs((mid_k, 7), (pass_q, 2)), 3: runs((pass_q, 1))},
        2: {2: runs((mid_k, 6)), 3: runs((end_k, 7))},
        4: {1: runs((mid_k, 5), (end_k, 6)), 2: runs((end_q, 6))},
        5: {2: runs((mid_k, 4), (end_k, 5))},
        6: {1: runs((mid_k, 3), (mid_q, 4), (end_k, 4))},
    }
    behind = {
        0: runs((pass_q, 4)),
        1: runs((mid_q, 7)),
        2: runs((mid_q, 6), (end_q, 7)),
        4: runs((mid_q, 5), (mid_q, 0)),
        5: runs((end_q, 5), (end_q, 0)),
    }

    def superstep(i, _):
        g = group(i)
        g1 = group(i + 1)

        def pair(j, _):
            for when, events in ahead.items():
                pl.when(i == when)(functools.partial(at, events, j))
            with jax.named_scope('two'):
                two(2 * j, 2 * g)
            return 0
        lax.fori_loop(0, g, pair, 0)
        with jax.named_scope('take_q'):
            for n in (0, 1):
                q_f(g1, n).wait_recv()
        with jax.named_scope('tail'):
            tail(g, g1)
        send_q(g)
        pl.when(i != 3)(functools.partial(send_k, g))
        for when, act in behind.items():
            pl.when(i == when)(act)
        return 0
    lax.fori_loop(0, NG - 1, superstep, 0)

    with jax.named_scope('two'):
        two(0, 2)
    finish_k(0, 0)
    finish_k(0, 1)
    send_k(0)
    mid_k(2)
    with jax.named_scope('tail'):
        tail(1)
    send_q(1)
    send_k(1)
    mid_k(0)
    mid_q(3)
    mid_k(1)
    end_k(3)
    end_q(4)
    mid_q(2)
    mid_q(1)
    end_k(2)
    end_k(0)
    end_q(3)
    end_k(1)
    end_q(2)
    end_q(1)

    for d in D3:
        ld_a(d).wait_send()
        ld_b(d).wait_send()
        q_b(7, d).wait_send()

    def sent_f(g, _):
        for n in (0, 1):
            q_n(g, n).wait_send()
            q_f(g, n).wait_send()
        return 0
    lax.fori_loop(0, 7, sent_f, 0)

    def sent_k(j, _):
        for d in D3:
            k_z(j, d).wait_send()
        for d in (0, 1, 2, 3):
            k_d(j, d).wait_send()
        return 0
    lax.fori_loop(0, KQ, sent_k, 0)

    def sent(g, _):
        r_d(g).wait_send()
        for d in D3:
            for f in (q_a, r_b, r_a, r_z):
                f(g, d).wait_send()
        return 0
    lax.fori_loop(0, NG, sent, 0)


def local(q, k, v, o, dout, lse):
    flat = (ROWS, HD)
    vm = pl.BlockSpec(memory_space=pltpu.VMEM)
    V, DMA = pltpu.VMEM, pltpu.SemaphoreType.DMA
    scratch = [
        V((NQ, 2, ROWS, HD), BF16), V((2, 4, 2, ROWS, HD), BF16), V((NQ, 4, 8, 128), F32),
        V((NQ, ROWS, HD), BF16), V((2, BQ, BK), F32),
        V((NC, 2 * HD, BK), BF16), V((NC, 2 * HD, BK), BF16), V((2, HD, BQ), BF16), V((2, HD, BQ), BF16),
        *[V((BQ, BK), BF16)] * 6,
        V((2, HD, BQ), F32), V((NC, HD, BK), F32), V((NC, HD, BK), F32),
        V((NG, NQ, GR, HD), F32), V((NG, 3, 4, GR, HD), F32), V((NG, 4, GR, HD), F32), V((NG, 3, GR, HD), F32),
        V((NG, 2, 4, 2, GR, HD), F32), V((NG, 4, 2, GR, HD), F32), V((NG, 4, 2, GR, HD), F32),
        V((NG, 3, 2, GR, HD), F32), V((ROWS, HD), BF16), V((1, ROWS), F32),
        DMA((6,)),
        *[DMA((3,))] * 4, *[DMA((NG, 3))] * 2, *[DMA((NG, 4))] * 2, *[DMA((KQ, 3))] * 2, *[DMA((KQ, 4))] * 2,
        *[DMA((NG, 3))] * 4, *[DMA((NG,))] * 2, *[DMA((NG, 3))] * 2,
    ]
    outs = pl.pallas_call(
        kernel,
        out_shape=[jax.ShapeDtypeStruct(flat, BF16)] * 3,
        in_specs=[pl.BlockSpec(memory_space=pl.ANY)] * 6, out_specs=[vm] * 3,
        scratch_shapes=scratch,
        compiler_params=pltpu.CompilerParams(collective_id=0, has_side_effects=True, vmem_limit_bytes=62 << 20),
    )(*[t.reshape(flat) for t in (q, k, v, o, dout)], lse)
    return tuple(t.reshape(ROWS, 1, HD) for t in outs)


def solution(mesh):
    rows = P(('data', 'cp'))
    cols = P(None, ('data', 'cp'))
    return jax.shard_map(local, mesh=mesh, in_specs=(rows, rows, rows, rows, rows, cols),
                         out_specs=(rows, rows, rows), check_vma=False)
```

time: 98.1 us -> 89.5 us (0.912)
  Pallas kernels: 94 us -> 85.5 us
    pallas_call x1, Pallas kernels: 94 us -> 85.5 us  [local(): pl.pallas_call(kernel, out_shape=[jax.ShapeDtypeStruct(flat, BF16)] * 3,...]
where the time goes in v1:
time: 89.5 us; the launch traced here: 89.3 us
  Pallas kernels  85.5 us (96%)
  local copies, waits for them, and re-layouts  3.21 us (4%)
    pallas_call x1, Pallas kernels, local(): pl.pallas_call(kernel, out_shape=[jax.ShapeDtypeStruct(flat, BF16)] * 3,...  85.5 us
    unnamed x7, local copies, waits for them, and re-layouts  3.21 us

profile of v1, /device:TPU:0, one launch (start us, length us, event | category | flops | bytes accessed | tf_op | source)
XLA Modules:
  0.0 89.3 jit_solution(7445160091942227482)
XLA Ops:
  0.6 85.5 %shard_map.85 = (bf16[512,128]{1,0:T(8,128)(2,1)}, bf16[512,128]{1,0:T(8,128)(2,1)}, bf16[512,128]{1,0:T(8,128)(2,1)}) custom-call(bf16[512,128]{1,0:T(8,128)(2,1)} %bitcast.8, bf16[512,128]{1,0:T(8,128)(2,1)} %bitcast.9, bf16[512,128]{1,0:T(8,128)(2,1)} %bitcast.10, bf16[512,128]{1,0:T(8,128)(2,1)} %bitcast.11, bf16[512,128]{1,0:T(8,128)(2,1)} %bitcast.12, ...), custom_call_target="tpu_custom_call" | custom-call | tf_op jit(solution)/shard_map/pallas_call | solution.py:486
  86.1 0.0 copy-start.1
  86.1 1.6 %copy.12 = bf16[512,1,128]{2,0,1:T(8,128)(2,1)} copy(bf16[512,1,128]{2,0,1:T(8,128)(2,1)} %bitcast.15) | data formatting | bytes 262144
  87.7 0.0 copy-done.1
  87.7 0.0 copy-start
  87.7 0.7 copy.13
  88.4 0.3 copy-done
  88.7 0.7 copy.14
Async XLA Ops:
  86.1 1.6 %copy-start.1 = (bf16[512,128]{1,0:T(8,128)(2,1)S(1)}, bf16[512,128]{1,0:T(8,128)(2,1)}, u32[]{:S(2)}) copy-start(bf16[512,128]{1,0:T(8,128)(2,1)} %get-tuple-element.7) | copy-start | bytes 393220
  87.7 1.0 %copy-start = (bf16[512,128]{1,0:T(8,128)(2,1)S(1)}, bf16[512,128]{1,0:T(8,128)(2,1)}, u32[]{:S(2)}) copy-start(bf16[512,128]{1,0:T(8,128)(2,1)} %get-tuple-element.8) | copy-start | bytes 393220

commit v2 on v1

v2 whole, which is shorter than its diff:
```python
import functools
import math

import jax
import jax.numpy as jnp
from jax import lax
from jax.experimental import pallas as pl
from jax.experimental.pallas import tpu as pltpu
from jax.sharding import PartitionSpec as P

F32, BF16 = jnp.float32, jnp.bfloat16
MESH = pl.DeviceIdType.MESH
ROWS, HD = 512, 128
L = 32
NC = ROWS // L
NG, GR = 8, 64
NQ, NK = 16, 8
BQ, BK = NQ * L, NK * L
KQ, KR = 4, 128
SCALE = HD ** -0.5
LOG2E = math.log2(math.e)


def dg(a, b, ca, cb):
    return lax.dot_general(a, b, (((ca,), (cb,)), ((), ())), preferred_element_type=F32)


def kernel(q_hbm, k_hbm, v_hbm, o_hbm, do_hbm, lse_hbm, dq_ref, dk_ref, dv_ref,
           qd, kv, ld, ex, thr, kt, vt, qt, dot, p_a, p_b, p_c, ds_a, ds_b, ds_c, dqt, dkt, dvt,
           pq, rb, sa, ra, pk, rd, sz, rz, o_in, lse_in,
           in_s, ld_s, qa_s, qb_s, kz_s, kd_s, rb_s, ra_s, rd_s, rz_s,
           lda_r, ldb_r, qa_r, q7_r, qn_r, qf_r, kz_r, kd_r, rb_r, ra_r, rd_r, rz_r):
    me = lax.axis_index('cp')
    core = lax.rem(me, 2)
    x = lax.rem(lax.div(me, 2), 4)
    y = lax.rem(lax.div(me, 8), 4)
    z = lax.div(me, 32)
    a = x + core * (y - x)
    b = y + core * (x - y)
    step_a, step_b = 2 + 6 * core, 8 - 6 * core

    def dev_q(b_, a_):
        return z * 32 + b_ * step_b + a_ * step_a + core

    def dev_k(z_, c_):
        return z_ * 32 + y * 8 + x * 2 + c_

    def turn(i, d):
        return lax.rem(i + d, 4)

    def remote(src, dst, ss, rs, dev):
        return pltpu.make_async_remote_copy(src_ref=src, dst_ref=dst, send_sem=ss, recv_sem=rs,
                                            device_id={'cp': dev}, device_id_type=MESH)

    D3 = (1, 2, 3)
    slot = b * 4 + a

    def rows_g(g):
        return pl.ds(pl.multiple_of(g * GR, GR), GR)

    def got(ref, sem):
        pltpu.make_async_copy(ref, ref, sem).wait()

    def own_a(src, ss, rs, d):
        return remote(src, src, ss, rs, dev_q(b, turn(a, d)))

    def to_b(src, ss, rs, d):
        return remote(src, src, ss, rs, dev_q(turn(b, d), a))

    def q_blk(n, g):
        return qd.at[b * 4 + turn(a, n), :, rows_g(g), :]

    def q_row(b_, g, n=0, size=4):
        return qd.at[pl.ds(b_ * 4 + n, size), :, rows_g(g), :]

    def q_n(g, n):
        return to_b(q_row(b, g), qb_s.at[0], qn_r.at[g], 1 + 2 * n)

    def q_f(g, n):
        return to_b(q_row(turn(b, 3 - 2 * n), g, 2 * n, 2), qb_s.at[0], qf_r.at[g], 1 + 2 * n)

    def k_z(j, d):
        r = kv.at[core, z, :, pl.ds(pl.multiple_of(j * KR, KR), KR), :]
        return remote(r, r, kz_s.at[0], kz_r.at[j], dev_k(turn(z, d), core))

    def k_d(j, d):
        r = kv.at[core, turn(z, 4 - d), :, pl.ds(pl.multiple_of(j * KR, KR), KR), :]
        return remote(r, r, kd_s.at[0], kd_r.at[j], dev_k(z, 1 - core))

    def r_b(g, d):
        return remote(pq.at[g, pl.ds(turn(b, d) * 4, 4)], rb.at[g, d - 1], rb_s.at[0], rb_r.at[g], dev_q(turn(b, d), a))

    def r_a(g, d):
        return remote(sa.at[g, turn(a, d)], ra.at[g, d - 1], ra_s.at[0], ra_r.at[g], dev_q(b, turn(a, d)))

    def r_d(g):
        return remote(pk.at[g, 1 - core], rd.at[g], rd_s.at[0], rd_r.at[g], dev_k(z, 1 - core))

    def r_z(g, d):
        return remote(sz.at[g, turn(z, d)], rz.at[g, d - 1], rz_s.at[0], rz_r.at[g], dev_k(turn(z, d), core))

    barrier = pltpu.get_barrier_semaphore()
    peers = [dev_q(b, turn(a, d)) for d in D3] + [dev_q(turn(b, d), a) for d in D3]
    peers += [dev_k(turn(z, d), core) for d in D3] + [dev_k(z, 1 - core)]
    for p in peers:
        pl.semaphore_signal(barrier, inc=1, device_id={'cp': p}, device_id_type=MESH)
    ins = [(do_hbm, qd.at[slot, 1], 0), (q_hbm, qd.at[slot, 0], 0), (k_hbm, kv.at[core, z, 0], 1),
           (v_hbm, kv.at[core, z, 1], 1), (o_hbm, o_in, 2), (lse_hbm, lse_in, 3)]
    for src, dst, n in ins:
        pltpu.make_async_copy(src, dst, in_s.at[n]).start()
    ld[slot] = jnp.zeros((4, 8, 128), F32)
    for ref, n in ((qd.at[slot], 0), (kv.at[core, z], 1), (o_in, 2), (lse_in, 3)):
        got(ref, in_s.at[n])

    def split(t):
        hi = t.astype(BF16).astype(F32)
        mid = (t - hi).astype(BF16).astype(F32)
        return hi, mid, t - hi - mid

    with jax.named_scope('own_ld'):
        for j in range(4):
            rows_j = pl.ds(j * 128, 128)
            d_j = jnp.sum(qd[slot, 1, rows_j, :].astype(F32) * o_in[rows_j, :].astype(F32), axis=1, keepdims=True)
            d_j = jnp.broadcast_to(d_j, (128, 128)).T[:1]
            for n, t in enumerate(split(lse_in[:, rows_j] * (-1.0 / SCALE)) + split(-d_j)):
                ld[slot, j, pl.ds(n, 1), :] = t
    with jax.named_scope('barrier'):
        pl.semaphore_wait(barrier, len(peers))

    def start_a(g):
        for d in D3:
            own_a(q_blk(0, g), qa_s.at[0], qa_r.at[g], d).start()

    for d in D3:
        own_a(ld.at[slot], ld_s.at[0], lda_r.at[0], d).start()
    for d in D3:
        k_z(0, d).start()
    k_d(0, 0).start()
    start_a(7)
    for d in D3:
        to_b(ld.at[slot], ld_s.at[0], ldb_r.at[0], d).start()
    for d in D3:
        to_b(q_blk(0, 7), qb_s.at[0], q7_r.at[0], d).start()

    def start_k(j, _):
        for d in D3:
            k_z(j, d).start()
        k_d(j, 0).start()
        return 0
    lax.fori_loop(1, KQ, start_k, 0)
    qi = lax.broadcasted_iota(jnp.int32, (BQ, 1), 0)
    ki = lax.broadcasted_iota(jnp.int32, (1, BK), 1)
    qpos = (qi & (L - 1)) * 128 + dev_q(qi >> 7, (qi >> 5) & 3)
    kpos = (ki & (L - 1)) * 128 + dev_k((ki >> 5) & 3, ki >> 7)
    thr[0] = jnp.full((BQ, BK), jnp.inf, F32)
    thr[1] = jnp.where(kpos <= qpos, jnp.inf, -jnp.inf).astype(F32)
    ex[...] = jnp.zeros_like(ex)
    ri = lax.broadcasted_iota(jnp.int32, (HD, BK), 0)
    for c in range(NC):
        kt[c, HD:] = jnp.where(ri < 3, 1.0, 0.0).astype(BF16)
        vt[c, HD:] = jnp.where((ri >= 3) & (ri < 6), 1.0, 0.0).astype(BF16)
    def got_a(g):
        got(qd.at[pl.ds(0, 3), :, rows_g(g), :], qa_r.at[g])

    def prep_e(i, _):
        for n in range(4):
            for j in range(4):
                ex[4 * i + n, pl.ds(j * 128, 128), pl.ds(0, 8)] = ld[4 * i + n, j].T.astype(BF16)
        return 0

    def pass_k(j):
        with jax.named_scope('pass_k'):
            got(kv.at[0, pl.ds(0, 3), :, pl.ds(0, KR), :], kz_r.at[j])
        for d in D3:
            k_d(j, d).start()

    with jax.named_scope('w_lda'):
        got(ld.at[pl.ds(0, 3)], lda_r.at[0])
    for n in D3:
        for d in D3:
            to_b(ld.at[b * 4 + turn(a, n)], ld_s.at[0], ldb_r.at[0], d).start()
    with jax.named_scope('got_a7'):
        got_a(7)
    for n in D3:
        for d in D3:
            to_b(q_blk(n, 7), qb_s.at[0], q7_r.at[0], d).start()
    dkt[...] = jnp.zeros_like(dkt)
    dvt[...] = jnp.zeros_like(dvt)
    dqt[...] = jnp.zeros_like(dqt)
    pass_k(0)
    with jax.named_scope('w_ldb'):
        got(ld.at[pl.ds(0, 12)], ldb_r.at[0])
    start_a(6)
    with jax.named_scope('prep_e'):
        lax.fori_loop(0, NQ // 4, prep_e, 0)
    start_a(5)

    def rows_q(which, r):
        return qd[:, which, pl.ds(pl.multiple_of(r * L, L), L), :].reshape(BQ, HD)

    def rows_k(which, c):
        return kv[:, :, which, pl.ds(pl.multiple_of(c * L, L), L), :].reshape(BK, HD)

    def rows_e(r):
        return ex[:, pl.ds(pl.multiple_of(r * L, L), L), :].reshape(BQ, HD)

    def take_k(j):
        with jax.named_scope('take_k'):
            got(kv.at[0, :, :, pl.ds(0, KR), :], kd_r.at[j])
        with jax.named_scope('prep_k'):
            for n in range(KR // L):
                c = j * (KR // L) + n
                kt[c, :HD] = rows_k(0, c).T
                vt[c, :HD] = rows_k(1, c).T

    def a_mm(r, c):
        e = rows_e(r)
        return (dg(jnp.concatenate([rows_q(0, r), e], axis=1), kt[c], 1, 0),
                dg(jnp.concatenate([rows_q(1, r), e], axis=1), vt[c], 1, 0))

    def a_vpu(sdp, diag, p_s, ds_s):
        s, dp = sdp
        t = s * (SCALE * LOG2E)
        if diag is not None:
            t = jnp.minimum(t, thr[diag])
        p = jnp.exp2(t)
        p_s[...] = p.astype(BF16)
        ds_s[...] = (p * dp).astype(BF16)

    def b_mm(c, h, p_s, ds_s):
        p, ds = p_s[...], ds_s[...]
        dqt[h] += dg(kt[c, :HD], ds, 1, 1)
        return dg(dot[h], p, 1, 0), dg(qt[h], ds, 1, 0)

    def q_prep(r, h):
        qt[h] = rows_q(0, r).T
        dot[h] = rows_q(1, r).T

    def finish_q(g, h):
        pq[g, :, pl.ds(h * L, L), :] = dqt[h].T.reshape(NQ, L, HD)
        dqt[h] = jnp.zeros((HD, BQ), F32)

    def finish_k(g, h):
        r = 2 * g + h
        pk[g, :, :, 0, pl.ds(h * L, L), :] = dkt[r].T.reshape(2, 4, L, HD)
        pk[g, :, :, 1, pl.ds(h * L, L), :] = dvt[r].T.reshape(2, 4, L, HD)

    def one(c, r0, d0):
        sdp = a_mm(r0, c + 1)
        dv, dk = b_mm(c, 0, p_a, ds_a)
        a_vpu(sdp, d0, p_a, ds_a)
        sdp = a_mm(r0 + 1, c + 1)
        dv1, dk1 = b_mm(c, 1, p_b, ds_b)
        a_vpu(sdp, None, p_b, ds_b)
        dvt[c] += dv + dv1
        dkt[c] += dk + dk1

    def two(c, r0):
        one(c, r0, None)
        one(c + 1, r0, lax.div(c + 2, r0))

    def tail(g, nxt=None):
        r0, r1 = 2 * g, 2 * g + 1
        sdp = a_mm(r1, r1)
        dv, dk = b_mm(r0, 0, p_a, ds_a)
        a_vpu(sdp, 1, p_c, ds_c)
        if nxt is not None:
            sdp = a_mm(2 * nxt, 0)
        dv1, dk1 = b_mm(r0, 1, p_b, ds_b)
        if nxt is not None:
            a_vpu(sdp, lax.div(7 - nxt, 7), p_a, ds_a)
        dvt[r0] += dv + dv1
        dkt[r0] += dk + dk1
        if nxt is not None:
            sdp = a_mm(2 * nxt + 1, 0)
        dv, dk = b_mm(r1, 1, p_c, ds_c)
        if nxt is not None:
            a_vpu(sdp, None, p_b, ds_b)
        dvt[r1] += dv
        dkt[r1] += dk
        finish_q(g, 0)
        finish_k(g, 0)
        finish_q(g, 1)
        finish_k(g, 1)
        if nxt is not None:
            q_prep(2 * nxt, 0)
            q_prep(2 * nxt + 1, 1)

    def send_q(g):
        for d in D3:
            r_b(g, d).start()

    def send_k(g):
        r_d(g).start()

    def mid_q(g):
        with jax.named_scope('mid_q'):
            got(rb.at[g], rb_r.at[g])
            sa[g] = pq[g, pl.ds(b * 4, 4)] + rb[g, 0] + rb[g, 1] + rb[g, 2]
        for d in D3:
            r_a(g, d).start()

    def mid_k(g):
        with jax.named_scope('mid_k'):
            got(rd.at[g], rd_r.at[g])
            sz[g] = pk[g, core] + rd[g]
        for d in D3:
            r_z(g, d).start()

    def end_q(g):
        with jax.named_scope('end_q'):
            got(ra.at[g], ra_r.at[g])
            dq = sa[g, a] + ra[g, 0] + ra[g, 1] + ra[g, 2]
            dq_ref[rows_g(g), :] = (dq * SCALE).astype(BF16)

    def end_k(g):
        with jax.named_scope('end_k'):
            got(rz.at[g], rz_r.at[g])
            dkv = sz[g, z] + rz[g, 0] + rz[g, 1] + rz[g, 2]
            dk_ref[rows_g(g), :] = (dkv[0] * SCALE).astype(BF16)
            dv_ref[rows_g(g), :] = dkv[1].astype(BF16)

    def pass_q(g):
        with jax.named_scope('pass_q'):
            got(q_row(0, g, 0, 8), qn_r.at[g])
        for n in (0, 1):
            q_f(g, n).start()

    def next_q(g):
        with jax.named_scope('next_q'):
            got_a(g)
        for n in (0, 1):
            q_n(g, n).start()

    take_k(0)
    with jax.named_scope('first_q'):
        got(q_row(0, 7, 0, 12), q7_r.at[0])
    q_prep(14, 0)
    q_prep(15, 1)
    with jax.named_scope('first'):
        a_vpu(a_mm(14, 0), None, p_a, ds_a)
        a_vpu(a_mm(15, 0), None, p_b, ds_b)
    next_q(6)
    for g in (0, 4, 3, 2, 1):
        start_a(g)
    pass_k(1)

    def group(i):
        late = lax.div(i + 4, 8)
        return 7 - i + late - 4 * (lax.div(i + 5, 8) - late)

    def at(events, j):
        for when, act in events.items():
            pl.when(j == when)(act)

    def runs(*acts):
        def run():
            for f, arg in acts:
                f(arg)
        return run

    ahead = {
        0: {1: runs((take_k, 1), (next_q, 5)), 2: runs((pass_k, 2), (next_q, 0)), 3: runs((take_k, 2), (next_q, 4)),
            4: runs((pass_k, 3), (pass_q, 6), (next_q, 3)), 5: runs((take_k, 3), (pass_q, 5), (next_q, 2)),
            6: runs((pass_q, 0), (next_q, 1))},
        1: {1: runs((pass_q, 3)), 2: runs((mid_k, 7), (pass_q, 2)), 3: runs((pass_q, 1))},
        2: {2: runs((mid_k, 6))},
        4: {1: runs((mid_k, 5))},
        5: {1: runs((mid_k, 4), (mid_q, 0))},
        6: {1: runs((mid_k, 3))},
    }
    behind = {
        0: runs((pass_q, 4)),
        1: runs((mid_q, 7)),
        2: runs((mid_q, 6)),
        4: runs((mid_q, 5)),
        6: runs((mid_q, 4)),
    }

    def superstep(i, _):
        g = group(i)
        g1 = group(i + 1)

        def pair(j, _):
            def at_some(whens):
                for when in whens:
                    pl.when(i == when)(functools.partial(at, ahead[when], j))
            pl.when(i < 2)(functools.partial(at_some, (0, 1)))
            pl.when(i >= 2)(functools.partial(at_some, (2, 4, 5, 6)))
            with jax.named_scope('two'):
                two(2 * j, 2 * g)
            return 0
        lax.fori_loop(0, g, pair, 0)
        with jax.named_scope('take_q'):
            got(q_row(0, g1), qf_r.at[g1])
        with jax.named_scope('tail'):
            tail(g, g1)
        send_q(g)
        pl.when(i != 3)(functools.partial(send_k, g))
        for when, act in behind.items():
            pl.when(i == when)(act)
        return 0
    lax.fori_loop(0, NG - 1, superstep, 0)

    with jax.named_scope('two'):
        two(0, 2)
    finish_k(0, 0)
    finish_k(0, 1)
    send_k(0)
    mid_k(2)
    with jax.named_scope('tail'):
        tail(1)
    send_q(1)
    send_k(1)
    mid_k(0)
    mid_q(3)
    mid_k(1)
    for g in (7, 6, 5):
        end_k(g)
        end_q(g)
    end_q(0)
    mid_q(2)
    end_k(4)
    end_q(4)
    mid_q(1)
    end_k(3)
    end_k(2)
    end_q(3)
    end_k(0)
    end_k(1)
    end_q(2)
    end_q(1)

    got(ld.at[pl.ds(0, 15)], ld_s.at[0])
    got(qd.at[pl.ds(0, 3)], qa_s.at[0])
    got(qd.at[pl.ds(0, 12)], qb_s.at[0])
    got(kv.at[0, pl.ds(0, 3)], kz_s.at[0])
    got(kv.at[0], kd_s.at[0])
    got(pq.at[pl.ds(0, 6)], rb_s.at[0])
    got(sa.at[pl.ds(0, 6)], ra_s.at[0])
    got(rd, rd_s.at[0])
    got(rz, rz_s.at[0])


def put(*refs):
    sem = refs[6]
    copies = [pltpu.make_async_copy(refs[n], refs[3 + n], sem.at[n]) for n in range(3)]
    for c in copies:
        c.start()
    for c in copies:
        c.wait()


def local(q, k, v, o, dout, lse):
    flat = (ROWS, HD)
    vm = pl.BlockSpec(memory_space=pltpu.VMEM)
    V, DMA = pltpu.VMEM, pltpu.SemaphoreType.DMA
    scratch = [
        V((NQ, 2, ROWS, HD), BF16), V((2, 4, 2, ROWS, HD), BF16), V((NQ, 4, 8, 128), F32),
        V((NQ, ROWS, HD), BF16), V((2, BQ, BK), F32),
        V((NC, 2 * HD, BK), BF16), V((NC, 2 * HD, BK), BF16), V((2, HD, BQ), BF16), V((2, HD, BQ), BF16),
        *[V((BQ, BK), BF16)] * 6,
        V((2, HD, BQ), F32), V((NC, HD, BK), F32), V((NC, HD, BK), F32),
        V((NG, NQ, GR, HD), F32), V((NG, 3, 4, GR, HD), F32), V((NG, 4, GR, HD), F32), V((NG, 3, GR, HD), F32),
        V((NG, 2, 4, 2, GR, HD), F32), V((NG, 4, 2, GR, HD), F32), V((NG, 4, 2, GR, HD), F32),
        V((NG, 3, 2, GR, HD), F32), V((ROWS, HD), BF16), V((1, ROWS), F32),
        DMA((4,)), *[DMA((1,))] * 9,
        DMA((1,)), DMA((1,)), DMA((NG,)), DMA((1,)), DMA((NG,)), DMA((NG,)), DMA((KQ,)), DMA((KQ,)), *[DMA((NG,))] * 4,
    ]
    outs = pl.pallas_call(
        kernel,
        out_shape=[pltpu.VMEM(flat, BF16)] * 3,
        in_specs=[pl.BlockSpec(memory_space=pl.ANY)] * 6, out_specs=[vm] * 3,
        scratch_shapes=scratch,
        compiler_params=pltpu.CompilerParams(collective_id=0, has_side_effects=True, vmem_limit_bytes=62 << 20),
    )(*[t.reshape(flat) for t in (q, k, v, o, dout)], lse)
    outs = pl.pallas_call(
        put,
        out_shape=[jax.ShapeDtypeStruct(flat, BF16)] * 3,
        in_specs=[vm] * 3, out_specs=[pl.BlockSpec(memory_space=pl.ANY)] * 3,
        scratch_shapes=[DMA((3,))],
    )(*[pltpu.with_memory_space_constraint(t, pltpu.VMEM) for t in outs])
    return tuple(t.reshape(ROWS, 1, HD) for t in outs)


def solution(mesh):
    rows = P(('data', 'cp'))
    cols = P(None, ('data', 'cp'))
    return jax.shard_map(local, mesh=mesh, in_specs=(rows, rows, rows, rows, rows, cols),
                         out_specs=(rows, rows, rows), check_vma=False)
```

time: 89.5 us -> 81.3 us (0.908)
  Pallas kernels: 85.5 us -> 80.5 us
  local copies, waits for them, and re-layouts: 3.21 us -> 0 us
    pallas_call x1 -> x2, Pallas kernels: 85.5 us -> 80.5 us  [the longest x1 79.7 us: local(): pl.pallas_call(kernel, out_shape=[pltpu.VMEM(flat, BF16)] * 3, in_specs=[...]
    unnamed x7 -> x0, local copies, waits for them, and re-layouts: 3.21 us -> none
where the time goes in v2:
time: 81.3 us; the launch traced here: 81.1 us
  Pallas kernels  80.5 us (99%)
    pallas_call x1, Pallas kernels, local(): pl.pallas_call(kernel, out_shape=[pltpu.VMEM(flat, BF16)] * 3, in_specs=[...  79.7 us

profile of v2, /device:TPU:0, one launch (start us, length us, event | category | flops | bytes accessed | tf_op | source)
XLA Modules:
  0.0 81.1 jit_solution(12382356006788139346)
XLA Ops:
  0.6 79.7 %shard_map.85 = (bf16[512,128]{1,0:T(8,128)(2,1)S(1)}, bf16[512,128]{1,0:T(8,128)(2,1)S(1)}, bf16[512,128]{1,0:T(8,128)(2,1)S(1)}) custom-call(bf16[512,128]{1,0:T(8,128)(2,1)} %bitcast.8, bf16[512,128]{1,0:T(8,128)(2,1)} %bitcast.9, bf16[512,128]{1,0:T(8,128)(2,1)} %bitcast.10, bf16[512,128]{1,0:T(8,128)(2,1)} %bitcast.11, bf16[512,128]{1,0:T(8,128)(2,1)} %bitcast.12, ...), custom_call_target="tpu_custom_call" | custom-call | tf_op jit(solution)/shard_map/pallas_call | solution.py:470
  80.4 0.8 shard_map.86

commit v3 on v2

--- a/solution.py
+++ b/solution.py
@@ -184,16 +184,15 @@
     for n in D3:
         for d in D3:
             to_b(q_blk(n, 7), qb_s.at[0], q7_r.at[0], d).start()
+    start_a(6)
     dkt[...] = jnp.zeros_like(dkt)
     dvt[...] = jnp.zeros_like(dvt)
     dqt[...] = jnp.zeros_like(dqt)
     pass_k(0)
     with jax.named_scope('w_ldb'):
         got(ld.at[pl.ds(0, 12)], ldb_r.at[0])
-    start_a(6)
     with jax.named_scope('prep_e'):
         lax.fori_loop(0, NQ // 4, prep_e, 0)
-    start_a(5)
 
     def rows_q(which, r):
         return qd[:, which, pl.ds(pl.multiple_of(r * L, L), L), :].reshape(BQ, HD)
@@ -333,17 +332,17 @@
             q_n(g, n).start()
 
     take_k(0)
+    pass_k(1)
     with jax.named_scope('first_q'):
         got(q_row(0, 7, 0, 12), q7_r.at[0])
     q_prep(14, 0)
     q_prep(15, 1)
+    next_q(6)
+    for g in (5, 0, 4, 3, 2, 1):
+        start_a(g)
     with jax.named_scope('first'):
         a_vpu(a_mm(14, 0), None, p_a, ds_a)
         a_vpu(a_mm(15, 0), None, p_b, ds_b)
-    next_q(6)
-    for g in (0, 4, 3, 2, 1):
-        start_a(g)
-    pass_k(1)
 
     def group(i):
         late = lax.div(i + 4, 8)
@@ -360,17 +359,17 @@
         return run
 
     ahead = {
-        0: {1: runs((take_k, 1), (next_q, 5)), 2: runs((pass_k, 2), (next_q, 0)), 3: runs((take_k, 2), (next_q, 4)),
-            4: runs((pass_k, 3), (pass_q, 6), (next_q, 3)), 5: runs((take_k, 3), (pass_q, 5), (next_q, 2)),
-            6: runs((pass_q, 0), (next_q, 1))},
-        1: {1: runs((pass_q, 3)), 2: runs((mid_k, 7), (pass_q, 2)), 3: runs((pass_q, 1))},
-        2: {2: runs((mid_k, 6))},
+        0: {1: runs((take_k, 1)), 2: runs((pass_k, 2)), 3: runs((take_k, 2), (next_q, 5)),
+            4: runs((pass_k, 3), (pass_q, 6), (next_q, 0)), 5: runs((take_k, 3), (next_q, 4)),
+            6: runs((next_q, 3))},
+        1: {1: runs((pass_q, 5), (next_q, 1)), 2: runs((mid_k, 7), (pass_q, 0)), 3: runs((pass_q, 4)), 4: runs((pass_q, 3))},
+        2: {1: runs((pass_q, 2)), 2: runs((mid_k, 6)), 3: runs((pass_q, 1))},
         4: {1: runs((mid_k, 5))},
-        5: {1: runs((mid_k, 4), (mid_q, 0))},
+        5: {1: runs((mid_k, 4)), 2: runs((mid_q, 0))},
         6: {1: runs((mid_k, 3))},
     }
     behind = {
-        0: runs((pass_q, 4)),
+        0: runs((next_q, 2)),
         1: runs((mid_q, 7)),
         2: runs((mid_q, 6)),
         4: runs((mid_q, 5)),

time: 81.3 us -> 76.5 us (0.941)
  Pallas kernels: 80.5 us -> 75.7 us
    pallas_call x1, Pallas kernels: 79.7 us -> 75 us  [local(): pl.pallas_call(kernel, out_shape=[pltpu.VMEM(flat, BF16)] * 3, in_specs=[...]
where the time goes in v3:
time: 76.5 us; the launch traced here: 76.4 us
  Pallas kernels  75.7 us (99%)
    pallas_call x1, Pallas kernels, local(): pl.pallas_call(kernel, out_shape=[pltpu.VMEM(flat, BF16)] * 3, in_specs=[...  75 us

profile of v3, /device:TPU:0, one launch (start us, length us, event | category | flops | bytes accessed | tf_op | source)
XLA Modules:
  0.0 76.4 jit_solution(3320845146999478222)
XLA Ops:
  0.6 75.0 %shard_map.85 = (bf16[512,128]{1,0:T(8,128)(2,1)S(1)}, bf16[512,128]{1,0:T(8,128)(2,1)S(1)}, bf16[512,128]{1,0:T(8,128)(2,1)S(1)}) custom-call(bf16[512,128]{1,0:T(8,128)(2,1)} %bitcast.8, bf16[512,128]{1,0:T(8,128)(2,1)} %bitcast.9, bf16[512,128]{1,0:T(8,128)(2,1)} %bitcast.10, bf16[512,128]{1,0:T(8,128)(2,1)} %bitcast.11, bf16[512,128]{1,0:T(8,128)(2,1)} %bitcast.12, ...), custom_call_target="tpu_custom_call" | custom-call | tf_op jit(solution)/shard_map/pallas_call | solution.py:469
  75.6 0.8 %shard_map.86 = (bf16[512,128]{1,0:T(8,128)(2,1)}, bf16[512,128]{1,0:T(8,128)(2,1)}, bf16[512,128]{1,0:T(8,128)(2,1)}) custom-call(bf16[512,128]{1,0:T(8,128)(2,1)S(1)} %get-tuple-element.9.refs_0_, bf16[512,128]{1,0:T(8,128)(2,1)S(1)} %get-tuple-element.10.refs_1_, bf16[512,128]{1,0:T(8,128)(2,1)S(1)} %get-tuple-element.11.refs_2_), custom_call_target="tpu_custom_call" | custom-call | tf_op jit(solution)/shard_map/pallas_call | solution.py:476

commit v4 on v3

--- a/solution.py
+++ b/solution.py
@@ -29,7 +29,7 @@
            qd, kv, ld, ex, thr, kt, vt, qt, dot, p_a, p_b, p_c, ds_a, ds_b, ds_c, dqt, dkt, dvt,
            pq, rb, sa, ra, pk, rd, sz, rz, o_in, lse_in,
            in_s, ld_s, qa_s, qb_s, kz_s, kd_s, rb_s, ra_s, rd_s, rz_s,
-           lda_r, ldb_r, qa_r, q7_r, qn_r, qf_r, kz_r, kd_r, rb_r, ra_r, rd_r, rz_r):
+           lda_r, ldb_r, qa_r, q7a_r, q7_r, qn_r, qf_r, kz_r, kd_r, rb_r, rf_r, ra_r, rd_r, rz_r, rzf_r):
     me = lax.axis_index('cp')
     core = lax.rem(me, 2)
     x = lax.rem(lax.div(me, 2), 4)
@@ -90,6 +90,18 @@
     def r_b(g, d):
         return remote(pq.at[g, pl.ds(turn(b, d) * 4, 4)], rb.at[g, d - 1], rb_s.at[0], rb_r.at[g], dev_q(turn(b, d), a))
 
+    def r_opp(g, n):
+        return remote(pq.at[g, pl.ds(turn(b, 2) * 4 + 2 * n, 2)], rb.at[g, 2, pl.ds(2 * n, 2)], rb_s.at[0], rb_r.at[g],
+                      dev_q(turn(b, 1 + 2 * n), a))
+
+    def r_near(g, n):
+        return remote(pq.at[g, pl.ds(turn(b, 1 + 2 * n) * 4 + 2 - 2 * n, 2)], rb.at[g, n, pl.ds(2 - 2 * n, 2)],
+                      rb_s.at[0], rf_r.at[g], dev_q(turn(b, 1 + 2 * n), a))
+
+    def r_on(g, n):
+        return remote(rb.at[g, 2, pl.ds(2 * n, 2)], rb.at[g, n, pl.ds(2 * n, 2)],
+                      rb_s.at[0], rf_r.at[g], dev_q(turn(b, 1 + 2 * n), a))
+
     def r_a(g, d):
         return remote(sa.at[g, turn(a, d)], ra.at[g, d - 1], ra_s.at[0], ra_r.at[g], dev_q(b, turn(a, d)))
 
@@ -98,6 +110,16 @@
 
     def r_z(g, d):
         return remote(sz.at[g, turn(z, d)], rz.at[g, d - 1], rz_s.at[0], rz_r.at[g], dev_k(turn(z, d), core))
+
+    def k_opp(g, n):
+        return remote(sz.at[g, turn(z, 2), n], rz.at[g, 2, n], rz_s.at[0], rz_r.at[g], dev_k(turn(z, 1 + 2 * n), core))
+
+    def k_near(g, n):
+        return remote(sz.at[g, turn(z, 1 + 2 * n), 1 - n], rz.at[g, n, 1 - n], rz_s.at[0], rzf_r.at[g],
+                      dev_k(turn(z, 1 + 2 * n), core))
+
+    def k_on(g, n):
+        return remote(rz.at[g, 2, n], rz.at[g, n, n], rz_s.at[0], rzf_r.at[g], dev_k(turn(z, 1 + 2 * n), core))
 
     barrier = pltpu.get_barrier_semaphore()
     peers = [dev_q(b, turn(a, d)) for d in D3] + [dev_q(turn(b, d), a) for d in D3]
@@ -136,7 +158,8 @@
     for d in D3:
         k_z(0, d).start()
     k_d(0, 0).start()
-    start_a(7)
+    for d in D3:
+        own_a(q_blk(0, 7), qa_s.at[0], q7a_r.at[a], d).start()
     for d in D3:
         to_b(ld.at[slot], ld_s.at[0], ldb_r.at[0], d).start()
     for d in D3:
@@ -179,11 +202,14 @@
     for n in D3:
         for d in D3:
             to_b(ld.at[b * 4 + turn(a, n)], ld_s.at[0], ldb_r.at[0], d).start()
-    with jax.named_scope('got_a7'):
-        got_a(7)
-    for n in D3:
-        for d in D3:
-            to_b(q_blk(n, 7), qb_s.at[0], q7_r.at[0], d).start()
+    for p in (0, 1, 3, 2):
+        @pl.when(a != p)
+        def _():
+            r = qd.at[b * 4 + p, :, rows_g(7), :]
+            with jax.named_scope('got_a7'):
+                got(r, q7a_r.at[p])
+            for d in D3:
+                to_b(r, qb_s.at[0], q7_r.at[0], d).start()
     start_a(6)
     dkt[...] = jnp.zeros_like(dkt)
     dvt[...] = jnp.zeros_like(dvt)
@@ -263,48 +289,76 @@
         sdp = a_mm(r1, r1)
         dv, dk = b_mm(r0, 0, p_a, ds_a)
         a_vpu(sdp, 1, p_c, ds_c)
+        dv1, dk1 = b_mm(r0, 1, p_b, ds_b)
+        dvt[r0] += dv + dv1
+        dkt[r0] += dk + dk1
+        finish_q(g, 0)
+        finish_k(g, 0)
         if nxt is not None:
             sdp = a_mm(2 * nxt, 0)
-        dv1, dk1 = b_mm(r0, 1, p_b, ds_b)
+        dv, dk = b_mm(r1, 1, p_c, ds_c)
         if nxt is not None:
             a_vpu(sdp, lax.div(7 - nxt, 7), p_a, ds_a)
-        dvt[r0] += dv + dv1
-        dkt[r0] += dk + dk1
+        dvt[r1] += dv
+        dkt[r1] += dk
         if nxt is not None:
             sdp = a_mm(2 * nxt + 1, 0)
-        dv, dk = b_mm(r1, 1, p_c, ds_c)
-        if nxt is not None:
-            a_vpu(sdp, None, p_b, ds_b)
-        dvt[r1] += dv
-        dkt[r1] += dk
-        finish_q(g, 0)
-        finish_k(g, 0)
         finish_q(g, 1)
         finish_k(g, 1)
         if nxt is not None:
+            a_vpu(sdp, None, p_b, ds_b)
             q_prep(2 * nxt, 0)
             q_prep(2 * nxt + 1, 1)
 
     def send_q(g):
+        for n in (0, 1):
+            r_opp(g, n).start()
+        for n in (0, 1):
+            r_near(g, n).start()
+
+    def relay_q(g):
+        with jax.named_scope('relay_q'):
+            got(rb.at[g, 2], rb_r.at[g])
+            for n in (0, 1):
+                half = pl.ds(2 * n, 2)
+                rb[g, 2, half] = rb[g, 2, half] + pq[g, pl.ds(turn(b, 1 + 2 * n) * 4 + 2 * n, 2)]
+        for n in (0, 1):
+            r_on(g, n).start()
+
+    def mid_q(g):
+        with jax.named_scope('mid_q'):
+            got(rb.at[g, pl.ds(0, 2)], rf_r.at[g])
+            sa[g] = pq[g, pl.ds(b * 4, 4)] + rb[g, 0] + rb[g, 1]
         for d in D3:
-            r_b(g, d).start()
+            r_a(g, d).start()
 
     def send_k(g):
         r_d(g).start()
 
-    def mid_q(g):
-        with jax.named_scope('mid_q'):
-            got(rb.at[g], rb_r.at[g])
-            sa[g] = pq[g, pl.ds(b * 4, 4)] + rb[g, 0] + rb[g, 1] + rb[g, 2]
-        for d in D3:
-            r_a(g, d).start()
-
-    def mid_k(g):
-        with jax.named_scope('mid_k'):
+    def sum_k(g):
+        with jax.named_scope('sum_k'):
             got(rd.at[g], rd_r.at[g])
             sz[g] = pk[g, core] + rd[g]
+
+    def mid_k(g):
+        sum_k(g)
         for d in D3:
             r_z(g, d).start()
+
+    def mid_k_by(g):
+        sum_k(g)
+        for n in (0, 1):
+            k_opp(g, n).start()
+        for n in (0, 1):
+            k_near(g, n).start()
+
+    def relay_k(g):
+        with jax.named_scope('relay_k'):
+            got(rz.at[g, 2], rz_r.at[g])
+            for n in (0, 1):
+                rz[g, 2, n] = rz[g, 2, n] + sz[g, turn(z, 1 + 2 * n), n]
+        for n in (0, 1):
+            k_on(g, n).start()
 
     def end_q(g):
         with jax.named_scope('end_q'):
@@ -312,12 +366,19 @@
             dq = sa[g, a] + ra[g, 0] + ra[g, 1] + ra[g, 2]
             dq_ref[rows_g(g), :] = (dq * SCALE).astype(BF16)
 
+    def out_k(g, dkv):
+        dk_ref[rows_g(g), :] = (dkv[0] * SCALE).astype(BF16)
+        dv_ref[rows_g(g), :] = dkv[1].astype(BF16)
+
     def end_k(g):
         with jax.named_scope('end_k'):
             got(rz.at[g], rz_r.at[g])
-            dkv = sz[g, z] + rz[g, 0] + rz[g, 1] + rz[g, 2]
-            dk_ref[rows_g(g), :] = (dkv[0] * SCALE).astype(BF16)
-            dv_ref[rows_g(g), :] = dkv[1].astype(BF16)
+            out_k(g, sz[g, z] + rz[g, 0] + rz[g, 1] + rz[g, 2])
+
+    def end_k_by(g):
+        with jax.named_scope('end_k_by'):
+            got(rz.at[g, pl.ds(0, 2)], rzf_r.at[g])
+            out_k(g, sz[g, z] + rz[g, 0] + rz[g, 1])
 
     def pass_q(g):
         with jax.named_scope('pass_q'):
@@ -333,13 +394,12 @@
 
     take_k(0)
     pass_k(1)
+    next_q(6)
     with jax.named_scope('first_q'):
         got(q_row(0, 7, 0, 12), q7_r.at[0])
     q_prep(14, 0)
     q_prep(15, 1)
-    next_q(6)
-    for g in (5, 0, 4, 3, 2, 1):
-        start_a(g)
+    start_a(5)
     with jax.named_scope('first'):
         a_vpu(a_mm(14, 0), None, p_a, ds_a)
         a_vpu(a_mm(15, 0), None, p_b, ds_b)
@@ -358,46 +418,58 @@
                 f(arg)
         return run
 
-    ahead = {
-        0: {1: runs((take_k, 1)), 2: runs((pass_k, 2)), 3: runs((take_k, 2), (next_q, 5)),
-            4: runs((pass_k, 3), (pass_q, 6), (next_q, 0)), 5: runs((take_k, 3), (next_q, 4)),
-            6: runs((next_q, 3))},
-        1: {1: runs((pass_q, 5), (next_q, 1)), 2: runs((mid_k, 7), (pass_q, 0)), 3: runs((pass_q, 4)), 4: runs((pass_q, 3))},
-        2: {1: runs((pass_q, 2)), 2: runs((mid_k, 6)), 3: runs((pass_q, 1))},
-        4: {1: runs((mid_k, 5))},
-        5: {1: runs((mid_k, 4)), 2: runs((mid_q, 0))},
-        6: {1: runs((mid_k, 3))},
+    ahead2 = {
+        6: {1: runs((mid_k_by, 3), (relay_q, 4), (mid_q, 0))},
+    }
+    ahead4 = {
+        0: {0: runs((take_k, 1), (pass_k, 2), (start_a, 0)),
+            1: runs((take_k, 2), (pass_k, 3), (pass_q, 6), (next_q, 5), (start_a, 4)),
+            2: runs((take_k, 3), (next_q, 0), (start_a, 3))},
+        1: {1: runs((mid_k, 7), (pass_q, 0), (next_q, 3), (start_a, 1)), 2: runs((next_q, 2))},
+        2: {1: runs((mid_k, 6), (pass_q, 3))},
+        4: {1: runs((mid_k, 5), (mid_q, 6))},
+        5: {0: runs((mid_k, 4), (relay_q, 0))},
     }
     behind = {
-        0: runs((next_q, 2)),
-        1: runs((mid_q, 7)),
-        2: runs((mid_q, 6)),
-        4: runs((mid_q, 5)),
-        6: runs((mid_q, 4)),
+        0: runs((pass_q, 5), (next_q, 4), (start_a, 2)),
+        1: runs((pass_q, 4), (next_q, 1), (relay_q, 7)),
+        2: runs((pass_q, 2), (relay_q, 6), (mid_q, 7)),
+        4: runs((pass_q, 1), (relay_q, 5)),
+        5: runs((mid_q, 5)),
     }
+
+    def fire(events, i, j):
+        for when, acts in events.items():
+            pl.when(i == when)(functools.partial(at, acts, j))
 
     def superstep(i, _):
         g = group(i)
         g1 = group(i + 1)
+        single = lax.rem(g, 2) + 2 * (lax.div(i + 2, 8) - lax.div(i + 1, 8))
 
         def pair(j, _):
-            def at_some(whens):
-                for when in whens:
-                    pl.when(i == when)(functools.partial(at, ahead[when], j))
-            pl.when(i < 2)(functools.partial(at_some, (0, 1)))
-            pl.when(i >= 2)(functools.partial(at_some, (2, 4, 5, 6)))
+            fire(ahead2, i, j)
             with jax.named_scope('two'):
                 two(2 * j, 2 * g)
             return 0
-        lax.fori_loop(0, g, pair, 0)
+
+        def double(j, _):
+            fire(ahead4, i, j)
+            with jax.named_scope('four'):
+                c = 2 * single + 4 * j
+                two(c, 2 * g)
+                two(c + 2, 2 * g)
+            return 0
+        lax.fori_loop(0, single, pair, 0)
+        lax.fori_loop(0, lax.div(g - single, 2), double, 0)
         with jax.named_scope('take_q'):
             got(q_row(0, g1), qf_r.at[g1])
         with jax.named_scope('tail'):
             tail(g, g1)
+        for when, act in behind.items():
+            pl.when(i == when)(act)
         send_q(g)
         pl.when(i != 3)(functools.partial(send_k, g))
-        for when, act in behind.items():
-            pl.when(i == when)(act)
         return 0
     lax.fori_loop(0, NG - 1, superstep, 0)
 
@@ -406,26 +478,37 @@
     finish_k(0, 0)
     finish_k(0, 1)
     send_k(0)
-    mid_k(2)
+    mid_k_by(2)
+    relay_q(3)
+    mid_q(4)
     with jax.named_scope('tail'):
         tail(1)
-    send_q(1)
+    for d in D3:
+        r_b(1, d).start()
     send_k(1)
-    mid_k(0)
+    mid_k_by(0)
+    relay_k(3)
+    mid_k(1)
+    relay_q(2)
     mid_q(3)
-    mid_k(1)
     for g in (7, 6, 5):
         end_k(g)
         end_q(g)
     end_q(0)
+    end_k(4)
+    relay_k(2)
+    relay_k(0)
+    with jax.named_scope('last_q'):
+        got(rb.at[1], rb_r.at[1])
+        sa[1] = pq[1, pl.ds(b * 4, 4)] + rb[1, 0] + rb[1, 1] + rb[1, 2]
+    for d in D3:
+        r_a(1, d).start()
     mid_q(2)
-    end_k(4)
     end_q(4)
-    mid_q(1)
-    end_k(3)
-    end_k(2)
+    end_k_by(3)
+    end_k_by(2)
     end_q(3)
-    end_k(0)
+    end_k_by(0)
     end_k(1)
     end_q(2)
     end_q(1)
@@ -464,7 +547,7 @@
         V((NG, 2, 4, 2, GR, HD), F32), V((NG, 4, 2, GR, HD), F32), V((NG, 4, 2, GR, HD), F32),
         V((NG, 3, 2, GR, HD), F32), V((ROWS, HD), BF16), V((1, ROWS), F32),
         DMA((4,)), *[DMA((1,))] * 9,
-        DMA((1,)), DMA((1,)), DMA((NG,)), DMA((1,)), DMA((NG,)), DMA((NG,)), DMA((KQ,)), DMA((KQ,)), *[DMA((NG,))] * 4,
+        DMA((1,)), DMA((1,)), DMA((NG,)), DMA((4,)), DMA((1,)), DMA((NG,)), DMA((NG,)), DMA((KQ,)), DMA((KQ,)), *[DMA((NG,))] * 6,
     ]
     outs = pl.pallas_call(
         kernel,

time: 76.5 us -> 75.5 us (0.987)
  Pallas kernels: 75.7 us -> 74.7 us
    pallas_call x1, Pallas kernels: 75 us -> 74 us  [local(): pl.pallas_call(kernel, out_shape=[pltpu.VMEM(flat, BF16)] * 3, in_specs=[...]
where the time goes in v4:
time: 75.5 us; the launch traced here: 75.4 us
  Pallas kernels  74.7 us (99%)
    pallas_call x1, Pallas kernels, local(): pl.pallas_call(kernel, out_shape=[pltpu.VMEM(flat, BF16)] * 3, in_specs=[...  74 us

profile of v4, /device:TPU:0, one launch (start us, length us, event | category | flops | bytes accessed | tf_op | source)
XLA Modules:
  0.0 75.4 jit_solution(11856207508180079227)
XLA Ops:
  0.6 74.0 %shard_map.85 = (bf16[512,128]{1,0:T(8,128)(2,1)S(1)}, bf16[512,128]{1,0:T(8,128)(2,1)S(1)}, bf16[512,128]{1,0:T(8,128)(2,1)S(1)}) custom-call(bf16[512,128]{1,0:T(8,128)(2,1)} %bitcast.8, bf16[512,128]{1,0:T(8,128)(2,1)} %bitcast.9, bf16[512,128]{1,0:T(8,128)(2,1)} %bitcast.10, bf16[512,128]{1,0:T(8,128)(2,1)} %bitcast.11, bf16[512,128]{1,0:T(8,128)(2,1)} %bitcast.12, ...), custom_call_target="tpu_custom_call" | custom-call | tf_op jit(solution)/shard_map/pallas_call | solution.py:552
  74.6 0.8 %shard_map.86 = (bf16[512,128]{1,0:T(8,128)(2,1)}, bf16[512,128]{1,0:T(8,128)(2,1)}, bf16[512,128]{1,0:T(8,128)(2,1)}) custom-call(bf16[512,128]{1,0:T(8,128)(2,1)S(1)} %get-tuple-element.9.refs_0_, bf16[512,128]{1,0:T(8,128)(2,1)S(1)} %get-tuple-element.10.refs_1_, bf16[512,128]{1,0:T(8,128)(2,1)S(1)} %get-tuple-element.11.refs_2_), custom_call_target="tpu_custom_call" | custom-call | tf_op jit(solution)/shard_map/pallas_call | solution.py:559

commit v5 on v4

v5 whole, which is shorter than its diff:
```python
import functools
import math

import jax
import jax.numpy as jnp
from jax import lax
from jax.experimental import pallas as pl
from jax.experimental.pallas import tpu as pltpu
from jax.sharding import PartitionSpec as P

F32, BF16 = jnp.float32, jnp.bfloat16
MESH = pl.DeviceIdType.MESH
ROWS, HD = 512, 128
L = 32
NC = ROWS // L
NG, GR = 8, 64
NQ, NK = 16, 8
BQ, BK = NQ * L, NK * L
KQ, KR = 4, 128
N4 = 4
D3, SIDES = (1, 2, 3), (0, 1)
SCALE = HD ** -0.5
LOG2E = math.log2(math.e)
SEQ = (7, 6, 0, 5, 4, 3, 2, 1)
END = 9
TAKE_K = (1, 2, 3)
PASS_K = (1, 2)
PASS_Q = (2, 9, 11, 19, 31, 32, 39)
NEXT_Q = (2, 3, 9, 11, 12, 19)
START_A = (1, 2, 3, 9, 11)
MID_K = (11, 31, 41, 51)
MID_K_BY = (61,)
RELAY_Q = (19, 39, 41, 49, 61)
MID_Q = (39, 49, 51, 61)


def dg(a, b, ca, cb):
    return lax.dot_general(a, b, (((ca,), (cb,)), ((), ())), preferred_element_type=F32)


def kernel(q_hbm, k_hbm, v_hbm, o_hbm, do_hbm, lse_hbm, dq_ref, dk_ref, dv_ref,
           qd, kv, ld, ex, thr, kt, vt, qt, dot, p_a, p_b, p_c, ds_a, ds_b, ds_c, dqt, dkt, dvt,
           pq, rb, sa, ra, pk, rd, sz, rz, o_in, lse_in,
           in_s, ld_s, qa_s, qb_s, kz_s, kd_s, rb_s, ra_s, rd_s, rz_s,
           lda_r, ldb_r, qa_r, q7a_r, q7_r, qn_r, qf_r, kz_r, kd_r, rb_r, rf_r, ra_r, rd_r, rz_r, rzf_r):
    me = lax.axis_index('cp')
    core = lax.rem(me, 2)
    x = lax.rem(lax.div(me, 2), 4)
    y = lax.rem(lax.div(me, 8), 4)
    z = lax.div(me, 32)
    a = x + core * (y - x)
    b = y + core * (x - y)
    step_a, step_b = 2 + 6 * core, 8 - 6 * core

    def dev_q(b_, a_):
        return z * 32 + b_ * step_b + a_ * step_a + core

    def dev_k(z_, c_):
        return z_ * 32 + y * 8 + x * 2 + c_

    def turn(i, d):
        return lax.rem(i + d, N4)

    def remote(src, dst, ss, rs, dev):
        return pltpu.make_async_remote_copy(src_ref=src, dst_ref=dst, send_sem=ss, recv_sem=rs,
                                            device_id={'cp': dev}, device_id_type=MESH)

    def side(i, n):
        return turn(i, 1 + 2 * n)

    def half(n, size=2):
        return pl.ds(2 * n, size)

    def row(b_, n=0, size=N4):
        return pl.ds(b_ * N4 + n, size)

    slot = b * N4 + a

    def rows_g(g):
        return pl.ds(pl.multiple_of(g * GR, GR), GR)

    def got(ref, sem):
        pltpu.make_async_copy(ref, ref, sem).wait()

    def own_a(src, ss, rs, d):
        return remote(src, src, ss, rs, dev_q(b, turn(a, d)))

    def to_b(src, ss, rs, d):
        return remote(src, src, ss, rs, dev_q(turn(b, d), a))

    def q_blk(n, g):
        return qd.at[b * N4 + turn(a, n), :, rows_g(g), :]

    def q_row(b_, g, n=0, size=N4):
        return qd.at[row(b_, n, size), :, rows_g(g), :]

    def q_n(g, n):
        return remote(q_row(b, g), q_row(b, g), qb_s, qn_r.at[g], dev_q(side(b, n), a))

    def q_f(g, n):
        r = q_row(side(b, 1 - n), g, 2 * n, 2)
        return remote(r, r, qb_s, qf_r.at[g], dev_q(side(b, n), a))

    def rows_p(j):
        return pl.ds(pl.multiple_of(j * KR, KR), KR)

    def k_z(j, d):
        r = kv.at[core, z, :, rows_p(j), :]
        return remote(r, r, kz_s, kz_r.at[j], dev_k(turn(z, d), core))

    def k_d(j, d=0):
        r = kv.at[core, turn(z, N4 - d), :, rows_p(j), :]
        return remote(r, r, kd_s, kd_r.at[j], dev_k(z, 1 - core))

    def r_b(g, d):
        return remote(pq.at[g, row(turn(b, d))], rb.at[g, d - 1], rb_s, rb_r.at[g], dev_q(turn(b, d), a))

    def r_opp(g, n):
        return remote(pq.at[g, row(turn(b, 2), 2 * n, 2)], rb.at[g, 2, half(n)], rb_s, rb_r.at[g], dev_q(side(b, n), a))

    def r_near(g, n):
        return remote(pq.at[g, row(side(b, n), 2 - 2 * n, 2)], rb.at[g, n, half(1 - n)], rb_s, rf_r.at[g],
                      dev_q(side(b, n), a))

    def r_on(g, n):
        return remote(rb.at[g, 2, half(n)], rb.at[g, n, half(n)], rb_s, rf_r.at[g], dev_q(side(b, n), a))

    def r_a(g, d):
        return remote(sa.at[g, turn(a, d)], ra.at[g, d - 1], ra_s, ra_r.at[g], dev_q(b, turn(a, d)))

    def r_d(g):
        return remote(pk.at[g, 1 - core], rd.at[g], rd_s, rd_r.at[g], dev_k(z, 1 - core))

    def r_z(g, d):
        return remote(sz.at[g, turn(z, d)], rz.at[g, d - 1], rz_s, rz_r.at[g], dev_k(turn(z, d), core))

    def k_opp(g, n):
        return remote(sz.at[g, turn(z, 2), n], rz.at[g, 2, n], rz_s, rz_r.at[g], dev_k(side(z, n), core))

    def k_near(g, n):
        return remote(sz.at[g, side(z, n), 1 - n], rz.at[g, n, 1 - n], rz_s, rzf_r.at[g], dev_k(side(z, n), core))

    def k_on(g, n):
        return remote(rz.at[g, 2, n], rz.at[g, n, n], rz_s, rzf_r.at[g], dev_k(side(z, n), core))

    def start(copy, g, which=D3):
        for n in which:
            copy(g, n).start()

    barrier = pltpu.get_barrier_semaphore()
    peers = [dev_q(b, turn(a, d)) for d in D3] + [dev_q(turn(b, d), a) for d in D3]
    peers += [dev_k(turn(z, d), core) for d in D3] + [dev_k(z, 1 - core)]
    for p in peers:
        pl.semaphore_signal(barrier, inc=1, device_id={'cp': p}, device_id_type=MESH)
    ins = [(do_hbm, qd.at[slot, 1], 0), (q_hbm, qd.at[slot, 0], 0), (k_hbm, kv.at[core, z, 0], 1),
           (v_hbm, kv.at[core, z, 1], 1), (o_hbm, o_in, 2), (lse_hbm, lse_in, 3)]
    for src, dst, n in ins:
        pltpu.make_async_copy(src, dst, in_s.at[n]).start()
    ld[slot] = jnp.zeros(ld.shape[1:], F32)
    for ref, n in ((qd.at[slot], 0), (kv.at[core, z], 1), (o_in, 2), (lse_in, 3)):
        got(ref, in_s.at[n])

    def split(t):
        hi = t.astype(BF16).astype(F32)
        mid = (t - hi).astype(BF16).astype(F32)
        return hi, mid, t - hi - mid

    with jax.named_scope('own_ld'):
        for j in range(N4):
            rows_j = rows_p(j)
            d_j = jnp.sum(qd[slot, 1, rows_j, :].astype(F32) * o_in[rows_j, :].astype(F32), axis=1, keepdims=True)
            d_j = jnp.broadcast_to(d_j, (KR, KR)).T[:1]
            for n, t in enumerate(split(lse_in[:, rows_j] * (-1.0 / SCALE)) + split(-d_j)):
                ld[slot, j, pl.ds(n, 1), :] = t
    with jax.named_scope('barrier'):
        pl.semaphore_wait(barrier, len(peers))

    def start_a(g):
        for d in D3:
            own_a(q_blk(0, g), qa_s, qa_r.at[g], d).start()

    for d in D3:
        own_a(ld.at[slot], ld_s, lda_r, d).start()
    for d in D3:
        own_a(q_blk(0, NG - 1), qa_s, q7a_r.at[a], d).start()
    start(k_z, 0)
    k_d(0).start()
    for d in D3:
        to_b(ld.at[slot], ld_s, ldb_r, d).start()
    for d in D3:
        to_b(q_blk(0, NG - 1), qb_s, q7_r, d).start()

    def start_k(j, _):
        start(k_z, j)
        k_d(j).start()
        return 0
    lax.fori_loop(1, KQ, start_k, 0)
    qi = lax.broadcasted_iota(jnp.int32, (BQ, 1), 0)
    ki = lax.broadcasted_iota(jnp.int32, (1, BK), 1)
    qpos = (qi & (L - 1)) * 128 + dev_q(qi >> 7, (qi >> 5) & 3)
    kpos = (ki & (L - 1)) * 128 + dev_k((ki >> 5) & 3, ki >> 7)
    thr[0] = jnp.full((BQ, BK), jnp.inf, F32)
    thr[1] = jnp.where(kpos <= qpos, jnp.inf, -jnp.inf).astype(F32)
    ex[...] = jnp.zeros_like(ex)
    ri = lax.broadcasted_iota(jnp.int32, (HD, BK), 0)
    for c in range(NC):
        kt[c, HD:] = jnp.where(ri < 3, 1.0, 0.0).astype(BF16)
        vt[c, HD:] = jnp.where((ri >= 3) & (ri < 6), 1.0, 0.0).astype(BF16)

    def got_a(g):
        got(q_row(0, g, 0, 3), qa_r.at[g])

    def prep_e(i, _):
        for n in range(N4):
            for j in range(N4):
                ex[N4 * i + n, pl.ds(j * KR, KR), pl.ds(0, 8)] = ld[N4 * i + n, j].T.astype(BF16)
        return 0

    def pass_k(j):
        with jax.named_scope('pass_k'):
            got(kv.at[0, pl.ds(0, 3), :, rows_p(0), :], kz_r.at[j])
        start(k_d, j)

    with jax.named_scope('w_lda'):
        got(ld.at[pl.ds(0, 3)], lda_r)
    for n in D3:
        for d in D3:
            to_b(ld.at[b * N4 + turn(a, n)], ld_s, ldb_r, d).start()
    for p in (0, 1, 3, 2):
        @pl.when(a != p)
        def _():
            r = qd.at[b * N4 + p, :, rows_g(NG - 1), :]
            with jax.named_scope('got_a7'):
                got(r, q7a_r.at[p])
            for d in D3:
                to_b(r, qb_s, q7_r, d).start()
    start_a(6)
    dkt[...] = jnp.zeros_like(dkt)
    dvt[...] = jnp.zeros_like(dvt)
    dqt[...] = jnp.zeros_like(dqt)
    pass_k(0)
    with jax.named_scope('w_ldb'):
        got(ld.at[pl.ds(0, 12)], ldb_r)
    with jax.named_scope('prep_e'):
        lax.fori_loop(0, NQ // N4, prep_e, 0)

    def rows_q(which, r):
        return qd[:, which, pl.ds(pl.multiple_of(r * L, L), L), :].reshape(BQ, HD)

    def rows_k(which, c):
        return kv[:, :, which, pl.ds(pl.multiple_of(c * L, L), L), :].reshape(BK, HD)

    def rows_e(r):
        return ex[:, pl.ds(pl.multiple_of(r * L, L), L), :].reshape(BQ, HD)

    def take_k(j):
        with jax.named_scope('take_k'):
            got(kv.at[0, :, :, rows_p(0), :], kd_r.at[j])
        with jax.named_scope('prep_k'):
            for n in range(KR // L):
                c = j * (KR // L) + n
                kt[c, :HD] = rows_k(0, c).T
                vt[c, :HD] = rows_k(1, c).T

    def a_mm(r, c):
        e = rows_e(r)
        return (dg(jnp.concatenate([rows_q(0, r), e], axis=1), kt[c], 1, 0),
                dg(jnp.concatenate([rows_q(1, r), e], axis=1), vt[c], 1, 0))

    def a_vpu(sdp, diag, p_s, ds_s):
        s, dp = sdp
        t = s * (SCALE * LOG2E)
        if diag is not None:
            t = jnp.minimum(t, thr[diag])
        p = jnp.exp2(t)
        p_s[...] = p.astype(BF16)
        ds_s[...] = (p * dp).astype(BF16)

    def b_mm(c, h, p_s, ds_s):
        p, ds = p_s[...], ds_s[...]
        dqt[h] += dg(kt[c, :HD], ds, 1, 1)
        return dg(dot[h], p, 1, 0), dg(qt[h], ds, 1, 0)

    def q_prep(r, h):
        qt[h] = rows_q(0, r).T
        dot[h] = rows_q(1, r).T

    def finish_q(g, h):
        pq[g, :, pl.ds(h * L, L), :] = dqt[h].T.reshape(NQ, L, HD)
        dqt[h] = jnp.zeros((HD, BQ), F32)

    def finish_k(g, h):
        r = 2 * g + h
        pk[g, :, :, 0, pl.ds(h * L, L), :] = dkt[r].T.reshape(2, N4, L, HD)
        pk[g, :, :, 1, pl.ds(h * L, L), :] = dvt[r].T.reshape(2, N4, L, HD)

    def one(c, r0, d0):
        sdp = a_mm(r0, c + 1)
        dv, dk = b_mm(c, 0, p_a, ds_a)
        a_vpu(sdp, d0, p_a, ds_a)
        sdp = a_mm(r0 + 1, c + 1)
        dv1, dk1 = b_mm(c, 1, p_b, ds_b)
        a_vpu(sdp, None, p_b, ds_b)
        dvt[c] += dv + dv1
        dkt[c] += dk + dk1

    def two(c, r0):
        one(c, r0, None)
        one(c + 1, r0, lax.div(c + 2, r0))

    def tail(g, nxt=None):
        r0, r1 = 2 * g, 2 * g + 1
        sdp = a_mm(r1, r1)
        dv, dk = b_mm(r0, 0, p_a, ds_a)
        a_vpu(sdp, 1, p_c, ds_c)
        dv1, dk1 = b_mm(r0, 1, p_b, ds_b)
        dvt[r0] += dv + dv1
        dkt[r0] += dk + dk1
        finish_q(g, 0)
        finish_k(g, 0)
        if nxt is not None:
            sdp = a_mm(2 * nxt, 0)
        dv, dk = b_mm(r1, 1, p_c, ds_c)
        if nxt is not None:
            a_vpu(sdp, lax.div(7 - nxt, 7), p_a, ds_a)
        dvt[r1] += dv
        dkt[r1] += dk
        if nxt is not None:
            sdp = a_mm(2 * nxt + 1, 0)
        finish_q(g, 1)
        finish_k(g, 1)
        if nxt is not None:
            a_vpu(sdp, None, p_b, ds_b)
            q_prep(2 * nxt, 0)
            q_prep(2 * nxt + 1, 1)

    def send_q(g):
        start(r_opp, g, SIDES)
        start(r_near, g, SIDES)

    def relay_q(g):
        with jax.named_scope('relay_q'):
            got(rb.at[g, 2], rb_r.at[g])
            for n in SIDES:
                rb[g, 2, half(n)] = rb[g, 2, half(n)] + pq[g, row(side(b, n), 2 * n, 2)]
        start(r_on, g, SIDES)

    def mid_q(g):
        with jax.named_scope('mid_q'):
            got(rb.at[g, half(0)], rf_r.at[g])
            sa[g] = pq[g, row(b)] + rb[g, 0] + rb[g, 1]
        start(r_a, g)

    def last_q(g):
        with jax.named_scope('last_q'):
            got(rb.at[g], rb_r.at[g])
            sa[g] = pq[g, row(b)] + rb[g, 0] + rb[g, 1] + rb[g, 2]
        start(r_a, g)

    def send_k(g):
        r_d(g).start()

    def sum_k(g):
        with jax.named_scope('sum_k'):
            got(rd.at[g], rd_r.at[g])
            sz[g] = pk[g, core] + rd[g]

    def mid_k(g):
        sum_k(g)
        start(r_z, g)

    def mid_k_by(g):
        sum_k(g)
        start(k_opp, g, SIDES)
        start(k_near, g, SIDES)

    def relay_k(g):
        with jax.named_scope('relay_k'):
            got(rz.at[g, 2], rz_r.at[g])
            for n in SIDES:
                rz[g, 2, n] = rz[g, 2, n] + sz[g, side(z, n), n]
        start(k_on, g, SIDES)

    def end_q(g):
        with jax.named_scope('end_q'):
            got(ra.at[g], ra_r.at[g])
            dq = sa[g, a] + ra[g, 0] + ra[g, 1] + ra[g, 2]
            dq_ref[rows_g(g), :] = (dq * SCALE).astype(BF16)

    def out_k(g, dkv):
        dk_ref[rows_g(g), :] = (dkv[0] * SCALE).astype(BF16)
        dv_ref[rows_g(g), :] = dkv[1].astype(BF16)

    def end_k(g):
        with jax.named_scope('end_k'):
            got(rz.at[g], rz_r.at[g])
            out_k(g, sz[g, z] + rz[g, 0] + rz[g, 1] + rz[g, 2])

    def end_k_by(g):
        with jax.named_scope('end_k_by'):
            got(rz.at[g, half(0)], rzf_r.at[g])
            out_k(g, sz[g, z] + rz[g, 0] + rz[g, 1])

    def pass_q(g):
        with jax.named_scope('pass_q'):
            got(q_row(0, g, 0, 2 * N4), qn_r.at[g])
        start(q_f, g, SIDES)

    def next_q(g):
        with jax.named_scope('next_q'):
            got_a(g)
        start(q_n, g, SIDES)

    take_k(0)
    pass_k(1)
    next_q(SEQ[1])
    with jax.named_scope('first_q'):
        got(q_row(0, NG - 1, 0, 12), q7_r)
    q_prep(NC - 2, 0)
    q_prep(NC - 1, 1)
    start_a(SEQ[2])
    with jax.named_scope('first'):
        a_vpu(a_mm(NC - 2, 0), None, p_a, ds_a)
        a_vpu(a_mm(NC - 1, 0), None, p_b, ds_b)

    def group(i):
        late = lax.div(i + 5, NG)
        return NG - 1 - i + late - 5 * (lax.div(i + 6, NG) - late)

    plan = {}
    for act, args, when in (
        (take_k, (1, 2, 3), TAKE_K),
        (pass_k, (2, 3), PASS_K),
        (pass_q, SEQ[1:], PASS_Q),
        (next_q, SEQ[2:], NEXT_Q),
        (start_a, SEQ[3:], START_A),
        (mid_k, (7, 6, 5, 4), MID_K),
        (mid_k_by, SEQ[5:], MID_K_BY),
        (relay_q, SEQ, RELAY_Q),
        (mid_q, SEQ, MID_Q),
    ):
        for arg, t in zip(args, when):
            plan.setdefault(t, []).append((act, arg))
    early = (pass_q, next_q, start_a)

    def fire(i, j, acts):
        for n in range(NG - 1):
            places = {t % 10: e for t, e in plan.items() if t // 10 == n}
            places = {t: [e for e in es if acts is None or (e[0] in early) == acts] for t, es in places.items()}
            if j is END:
                places = {t: es for t, es in places.items() if t == END and es}
            else:
                places = {t: es for t, es in places.items() if t != END and es}
            if places:
                pl.when(i == n)(functools.partial(at, j, places))

    def at(j, places):
        for t, es in places.items():
            def run(es=es):
                for act, arg in es:
                    act(arg)
            if j is END:
                run()
            else:
                pl.when(j == t)(run)

    def superstep(i, _):
        g = group(i)
        g1 = group(i + 1)
        single = lax.rem(g, 2) + 2 * (lax.div(i + 2, NG) - lax.div(i + 1, NG))

        def pair(j, _):
            fire(i, j, None)
            with jax.named_scope('two'):
                two(2 * j, 2 * g)
            return 0

        def double(j, _):
            fire(i, j + single, None)
            with jax.named_scope('four'):
                c = 2 * single + N4 * j
                two(c, 2 * g)
                two(c + 2, 2 * g)
            return 0
        lax.fori_loop(0, single, pair, 0)
        lax.fori_loop(0, lax.div(g - single, 2), double, 0)
        with jax.named_scope('take_q'):
            got(q_row(0, g1), qf_r.at[g1])
        with jax.named_scope('tail'):
            tail(g, g1)
        fire(i, END, True)
        send_q(g)
        pl.when(i != 2)(functools.partial(send_k, g))
        fire(i, END, False)
        return 0
    lax.fori_loop(0, NG - 1, superstep, 0)

    with jax.named_scope('two'):
        two(0, 2)
    finish_k(0, 0)
    finish_k(0, 1)
    send_k(0)
    mid_k_by(2)
    relay_q(3)
    with jax.named_scope('tail'):
        tail(1)
    start(r_b, 1)
    send_k(1)
    mid_k_by(0)
    relay_k(3)
    mid_k(1)
    relay_q(2)
    mid_q(4)
    mid_q(3)
    for g in (7, 6, 5):
        end_k(g)
        end_q(g)
    end_q(0)
    end_k(4)
    relay_k(2)
    relay_k(0)
    last_q(1)
    mid_q(2)
    end_q(4)
    end_k_by(3)
    end_k_by(2)
    end_q(3)
    end_k_by(0)
    end_k(1)
    end_q(2)
    end_q(1)

    got(ld.at[pl.ds(0, 15)], ld_s)
    got(qd.at[pl.ds(0, 3)], qa_s)
    got(qd.at[pl.ds(0, 12)], qb_s)
    got(kv.at[0, pl.ds(0, 3)], kz_s)
    got(kv.at[0], kd_s)
    got(pq.at[pl.ds(0, 6)], rb_s)
    got(sa.at[pl.ds(0, 6)], ra_s)
    got(rd, rd_s)
    got(rz, rz_s)


def put(*refs):
    sem = refs[6]
    copies = [pltpu.make_async_copy(refs[n], refs[3 + n], sem.at[n]) for n in range(3)]
    for c in copies:
        c.start()
    for c in copies:
        c.wait()


def local(q, k, v, o, dout, lse):
    flat = (ROWS, HD)
    vm = pl.BlockSpec(memory_space=pltpu.VMEM)
    V, DMA = pltpu.VMEM, pltpu.SemaphoreType.DMA
    scratch = [
        V((NQ, 2, ROWS, HD), BF16), V((2, 4, 2, ROWS, HD), BF16), V((NQ, 4, 8, 128), F32),
        V((NQ, ROWS, HD), BF16), V((2, BQ, BK), F32),
        V((NC, 2 * HD, BK), BF16), V((NC, 2 * HD, BK), BF16), V((2, HD, BQ), BF16), V((2, HD, BQ), BF16),
        *[V((BQ, BK), BF16)] * 6,
        V((2, HD, BQ), F32), V((NC, HD, BK), F32), V((NC, HD, BK), F32),
        V((NG, NQ, GR, HD), F32), V((NG, 3, 4, GR, HD), F32), V((NG, 4, GR, HD), F32), V((NG, 3, GR, HD), F32),
        V((NG, 2, 4, 2, GR, HD), F32), V((NG, 4, 2, GR, HD), F32), V((NG, 4, 2, GR, HD), F32),
        V((NG, 3, 2, GR, HD), F32), V((ROWS, HD), BF16), V((1, ROWS), F32),
        DMA((N4,)), *[DMA] * 9,
        DMA, DMA, DMA((NG,)), DMA((N4,)), DMA, DMA((NG,)), DMA((NG,)), DMA((KQ,)), DMA((KQ,)), *[DMA((NG,))] * 6,
    ]
    outs = pl.pallas_call(
        kernel,
        out_shape=[pltpu.VMEM(flat, BF16)] * 3,
        in_specs=[pl.BlockSpec(memory_space=pl.ANY)] * 6, out_specs=[vm] * 3,
        scratch_shapes=scratch,
        compiler_params=pltpu.CompilerParams(collective_id=0, has_side_effects=True, vmem_limit_bytes=62 << 20),
    )(*[t.reshape(flat) for t in (q, k, v, o, dout)], lse)
    outs = pl.pallas_call(
        put,
        out_shape=[jax.ShapeDtypeStruct(flat, BF16)] * 3,
        in_specs=[vm] * 3, out_specs=[pl.BlockSpec(memory_space=pl.ANY)] * 3,
        scratch_shapes=[DMA((3,))],
    )(*[pltpu.with_memory_space_constraint(t, pltpu.VMEM) for t in outs])
    return tuple(t.reshape(ROWS, 1, HD) for t in outs)


def solution(mesh):
    rows = P(('data', 'cp'))
    cols = P(None, ('data', 'cp'))
    return jax.shard_map(local, mesh=mesh, in_specs=(rows, rows, rows, rows, rows, cols),
                         out_specs=(rows, rows, rows), check_vma=False)
```

time: 75.5 us -> 74.2 us (0.983)
  Pallas kernels: 74.7 us -> 73.4 us
    pallas_call x1, Pallas kernels: 74 us -> 72.7 us  [local(): pl.pallas_call(kernel, out_shape=[pltpu.VMEM(flat, BF16)] * 3, in_specs=[...]
where the time goes in v5:
time: 74.2 us; the launch traced here: 74.1 us
  Pallas kernels  73.4 us (99%)
    pallas_call x1, Pallas kernels, local(): pl.pallas_call(kernel, out_shape=[pltpu.VMEM(flat, BF16)] * 3, in_specs=[...  72.7 us

profile of v5, /device:TPU:0, one launch (start us, length us, event | category | flops | bytes accessed | tf_op | source)
XLA Modules:
  0.0 74.1 jit_solution(16636923576182845077)
XLA Ops:
  0.6 72.7 %shard_map.85 = (bf16[512,128]{1,0:T(8,128)(2,1)S(1)}, bf16[512,128]{1,0:T(8,128)(2,1)S(1)}, bf16[512,128]{1,0:T(8,128)(2,1)S(1)}) custom-call(bf16[512,128]{1,0:T(8,128)(2,1)} %bitcast.8, bf16[512,128]{1,0:T(8,128)(2,1)} %bitcast.9, bf16[512,128]{1,0:T(8,128)(2,1)} %bitcast.10, bf16[512,128]{1,0:T(8,128)(2,1)} %bitcast.11, bf16[512,128]{1,0:T(8,128)(2,1)} %bitcast.12, ...), custom_call_target="tpu_custom_call" | custom-call | tf_op jit(solution)/shard_map/pallas_call | solution.py:569
  73.3 0.8 %shard_map.86 = (bf16[512,128]{1,0:T(8,128)(2,1)}, bf16[512,128]{1,0:T(8,128)(2,1)}, bf16[512,128]{1,0:T(8,128)(2,1)}) custom-call(bf16[512,128]{1,0:T(8,128)(2,1)S(1)} %get-tuple-element.9.refs_0_, bf16[512,128]{1,0:T(8,128)(2,1)S(1)} %get-tuple-element.10.refs_1_, bf16[512,128]{1,0:T(8,128)(2,1)S(1)} %get-tuple-element.11.refs_2_), custom_call_target="tpu_custom_call" | custom-call | tf_op jit(solution)/shard_map/pallas_call | solution.py:576

commit v6 on v5

--- a/solution.py
+++ b/solution.py
@@ -18,20 +18,20 @@
 BQ, BK = NQ * L, NK * L
 KQ, KR = 4, 128
 N4 = 4
+TERMS = 24
 D3, SIDES = (1, 2, 3), (0, 1)
 SCALE = HD ** -0.5
 LOG2E = math.log2(math.e)
-SEQ = (7, 6, 0, 5, 4, 3, 2, 1)
+SEQ = (7, 6, 0, 5, 1, 4, 3, 2)
 END = 9
 TAKE_K = (1, 2, 3)
 PASS_K = (1, 2)
-PASS_Q = (2, 9, 11, 19, 31, 32, 39)
-NEXT_Q = (2, 3, 9, 11, 12, 19)
-START_A = (1, 2, 3, 9, 11)
-MID_K = (11, 31, 41, 51)
-MID_K_BY = (61,)
-RELAY_Q = (19, 39, 41, 49, 61)
-MID_Q = (39, 49, 51, 61)
+PASS_Q = (3, 9, 11, 19, 31, 32)
+NEXT_Q = (2, 3, 9, 11, 12)
+START_A = (1, 2, 3, 9)
+MID_K = (11, 31, 49, 61)
+RELAY_Q = (19, 39, 49, 51, 59)
+MID_Q = (39, 59, 60, 61)
 
 
 def dg(a, b, ca, cb):
@@ -156,22 +156,15 @@
            (v_hbm, kv.at[core, z, 1], 1), (o_hbm, o_in, 2), (lse_hbm, lse_in, 3)]
     for src, dst, n in ins:
         pltpu.make_async_copy(src, dst, in_s.at[n]).start()
-    ld[slot] = jnp.zeros(ld.shape[1:], F32)
     for ref, n in ((qd.at[slot], 0), (kv.at[core, z], 1), (o_in, 2), (lse_in, 3)):
         got(ref, in_s.at[n])
-
-    def split(t):
-        hi = t.astype(BF16).astype(F32)
-        mid = (t - hi).astype(BF16).astype(F32)
-        return hi, mid, t - hi - mid
 
     with jax.named_scope('own_ld'):
         for j in range(N4):
             rows_j = rows_p(j)
             d_j = jnp.sum(qd[slot, 1, rows_j, :].astype(F32) * o_in[rows_j, :].astype(F32), axis=1, keepdims=True)
-            d_j = jnp.broadcast_to(d_j, (KR, KR)).T[:1]
-            for n, t in enumerate(split(lse_in[:, rows_j] * (-1.0 / SCALE)) + split(-d_j)):
-                ld[slot, j, pl.ds(n, 1), :] = t
+            ld[slot, pl.ds(j, 1), :] = lse_in[:, rows_j] * (-1.0 / SCALE)
+            ld[slot, pl.ds(N4 + j, 1), :] = -jnp.broadcast_to(d_j, (KR, KR)).T[:1]
     with jax.named_scope('barrier'):
         pl.semaphore_wait(barrier, len(peers))
 
@@ -181,14 +174,17 @@
 
     for d in D3:
         own_a(ld.at[slot], ld_s, lda_r, d).start()
+    start(k_z, 0)
     for d in D3:
         own_a(q_blk(0, NG - 1), qa_s, q7a_r.at[a], d).start()
-    start(k_z, 0)
     k_d(0).start()
     for d in D3:
         to_b(ld.at[slot], ld_s, ldb_r, d).start()
     for d in D3:
         to_b(q_blk(0, NG - 1), qb_s, q7_r, d).start()
+
+    start_a(SEQ[1])
+    start_a(SEQ[2])
 
     def start_k(j, _):
         start(k_z, j)
@@ -203,17 +199,23 @@
     thr[1] = jnp.where(kpos <= qpos, jnp.inf, -jnp.inf).astype(F32)
     ex[...] = jnp.zeros_like(ex)
     ri = lax.broadcasted_iota(jnp.int32, (HD, BK), 0)
+    of_d = ((ri >> 2) & 1) == 1
     for c in range(NC):
-        kt[c, HD:] = jnp.where(ri < 3, 1.0, 0.0).astype(BF16)
-        vt[c, HD:] = jnp.where((ri >= 3) & (ri < 6), 1.0, 0.0).astype(BF16)
+        kt[c, HD:] = jnp.where((ri < TERMS) & ~of_d, 1.0, 0.0).astype(BF16)
+        vt[c, HD:] = jnp.where((ri < TERMS) & of_d, 1.0, 0.0).astype(BF16)
 
     def got_a(g):
         got(q_row(0, g, 0, 3), qa_r.at[g])
 
     def prep_e(i, _):
         for n in range(N4):
+            t = ld[N4 * i + n]
+            hi = t.astype(BF16).astype(F32)
+            mid = (t - hi).astype(BF16).astype(F32)
+            terms = jnp.concatenate([hi, mid, t - hi - mid], axis=0).T
+            quarter = lax.broadcasted_iota(jnp.int32, terms.shape, 1) & 3
             for j in range(N4):
-                ex[N4 * i + n, pl.ds(j * KR, KR), pl.ds(0, 8)] = ld[N4 * i + n, j].T.astype(BF16)
+                ex[N4 * i + n, rows_p(j), pl.ds(0, TERMS)] = jnp.where(quarter == j, terms, 0.0).astype(BF16)
         return 0
 
     def pass_k(j):
@@ -234,7 +236,6 @@
                 got(r, q7a_r.at[p])
             for d in D3:
                 to_b(r, qb_s, q7_r, d).start()
-    start_a(6)
     dkt[...] = jnp.zeros_like(dkt)
     dvt[...] = jnp.zeros_like(dvt)
     dqt[...] = jnp.zeros_like(dqt)
@@ -412,30 +413,31 @@
         start(q_n, g, SIDES)
 
     take_k(0)
-    pass_k(1)
-    next_q(SEQ[1])
+    got_a(SEQ[1])
+    for d in D3:
+        to_b(q_row(b, SEQ[1]), qb_s, qf_r.at[SEQ[1]], d).start()
     with jax.named_scope('first_q'):
         got(q_row(0, NG - 1, 0, 12), q7_r)
     q_prep(NC - 2, 0)
     q_prep(NC - 1, 1)
-    start_a(SEQ[2])
+    next_q(SEQ[2])
+    start_a(SEQ[3])
     with jax.named_scope('first'):
         a_vpu(a_mm(NC - 2, 0), None, p_a, ds_a)
         a_vpu(a_mm(NC - 1, 0), None, p_b, ds_b)
+    pass_k(1)
 
     def group(i):
-        late = lax.div(i + 5, NG)
-        return NG - 1 - i + late - 5 * (lax.div(i + 6, NG) - late)
+        return SEQ[0] + sum((SEQ[n] - SEQ[n - 1]) * lax.div(i + NG - n, NG) for n in range(1, NG))
 
     plan = {}
     for act, args, when in (
         (take_k, (1, 2, 3), TAKE_K),
         (pass_k, (2, 3), PASS_K),
-        (pass_q, SEQ[1:], PASS_Q),
-        (next_q, SEQ[2:], NEXT_Q),
-        (start_a, SEQ[3:], START_A),
+        (pass_q, SEQ[2:], PASS_Q),
+        (next_q, SEQ[3:], NEXT_Q),
+        (start_a, SEQ[4:], START_A),
         (mid_k, (7, 6, 5, 4), MID_K),
-        (mid_k_by, SEQ[5:], MID_K_BY),
         (relay_q, SEQ, RELAY_Q),
         (mid_q, SEQ, MID_Q),
     ):
@@ -467,7 +469,7 @@
     def superstep(i, _):
         g = group(i)
         g1 = group(i + 1)
-        single = lax.rem(g, 2) + 2 * (lax.div(i + 2, NG) - lax.div(i + 1, NG))
+        single = lax.rem(g, 2)
 
         def pair(j, _):
             fire(i, j, None)
@@ -475,60 +477,84 @@
                 two(2 * j, 2 * g)
             return 0
 
+        def four(j):
+            c = 2 * single + N4 * j
+            two(c, 2 * g)
+            two(c + 2, 2 * g)
+
         def double(j, _):
             fire(i, j + single, None)
             with jax.named_scope('four'):
-                c = 2 * single + N4 * j
-                two(c, 2 * g)
-                two(c + 2, 2 * g)
+                four(j)
             return 0
+
+        def last():
+            with jax.named_scope('take_q'):
+                pl.when(i == 0)(lambda: got(q_row(0, g1, 0, 12), qf_r.at[g1]))
+                pl.when(i > 0)(lambda: got(q_row(0, g1), qf_r.at[g1]))
+
+        fours = lax.div(g - single, 2)
         lax.fori_loop(0, single, pair, 0)
-        lax.fori_loop(0, lax.div(g - single, 2), double, 0)
-        with jax.named_scope('take_q'):
-            got(q_row(0, g1), qf_r.at[g1])
-        with jax.named_scope('tail'):
-            tail(g, g1)
+        lax.fori_loop(0, fours - 1, double, 0)
+
+        @pl.when(fours > 0)
+        def _():
+            fire(i, fours - 1 + single, None)
+            last()
+            with jax.named_scope('fourtail'):
+                four(fours - 1)
+                tail(g, g1)
+
+        @pl.when(fours == 0)
+        def _():
+            last()
+            with jax.named_scope('tail'):
+                tail(g, g1)
         fire(i, END, True)
-        send_q(g)
-        pl.when(i != 2)(functools.partial(send_k, g))
+        pl.when(i <= N4)(functools.partial(send_q, g))
+        pl.when(i > N4)(functools.partial(start, r_b, g))
+        pl.when((i != SEQ.index(0)) & (i != SEQ.index(1)))(functools.partial(send_k, g))
         fire(i, END, False)
         return 0
     lax.fori_loop(0, NG - 1, superstep, 0)
 
-    with jax.named_scope('two'):
-        two(0, 2)
-    finish_k(0, 0)
-    finish_k(0, 1)
-    send_k(0)
-    mid_k_by(2)
-    relay_q(3)
+    def close(g):
+        with jax.named_scope('two'):
+            two(2 * g, N4)
+        for h in SIDES:
+            finish_k(g, h)
+        send_k(g)
+
+    close(0)
+    mid_k_by(3)
+    close(1)
+    mid_k_by(0)
+    mid_q(1)
+    last_q(4)
     with jax.named_scope('tail'):
-        tail(1)
-    start(r_b, 1)
-    send_k(1)
-    mid_k_by(0)
+        tail(2)
+    start(r_b, 2)
+    send_k(2)
+    mid_k_by(1)
+    mid_k(2)
     relay_k(3)
-    mid_k(1)
-    relay_q(2)
-    mid_q(4)
-    mid_q(3)
+    relay_k(0)
+    last_q(3)
+    relay_k(1)
     for g in (7, 6, 5):
         end_k(g)
         end_q(g)
     end_q(0)
+    end_q(1)
     end_k(4)
-    relay_k(2)
-    relay_k(0)
-    last_q(1)
-    mid_q(2)
+    last_q(2)
+    end_k_by(3)
     end_q(4)
-    end_k_by(3)
-    end_k_by(2)
     end_q(3)
     end_k_by(0)
-    end_k(1)
+    end_k_by(1)
+    end_k(2)
     end_q(2)
-    end_q(1)
 
     got(ld.at[pl.ds(0, 15)], ld_s)
     got(qd.at[pl.ds(0, 3)], qa_s)
@@ -555,7 +581,7 @@
     vm = pl.BlockSpec(memory_space=pltpu.VMEM)
     V, DMA = pltpu.VMEM, pltpu.SemaphoreType.DMA
     scratch = [
-        V((NQ, 2, ROWS, HD), BF16), V((2, 4, 2, ROWS, HD), BF16), V((NQ, 4, 8, 128), F32),
+        V((NQ, 2, ROWS, HD), BF16), V((2, 4, 2, ROWS, HD), BF16), V((NQ, 8, 128), F32),
         V((NQ, ROWS, HD), BF16), V((2, BQ, BK), F32),
         V((NC, 2 * HD, BK), BF16), V((NC, 2 * HD, BK), BF16), V((2, HD, BQ), BF16), V((2, HD, BQ), BF16),
         *[V((BQ, BK), BF16)] * 6,

time: 74.2 us -> 72.2 us (0.973)
  Pallas kernels: 73.4 us -> 71.3 us
    pallas_call x1, Pallas kernels: 72.7 us -> 70.5 us  [local(): pl.pallas_call(kernel, out_shape=[pltpu.VMEM(flat, BF16)] * 3, in_specs=[...]
where the time goes in v6:
time: 72.2 us; the launch traced here: 72.1 us
  Pallas kernels  71.3 us (99%)
  between operations  0.8 us (1%)
    pallas_call x1, Pallas kernels, local(): pl.pallas_call(kernel, out_shape=[pltpu.VMEM(flat, BF16)] * 3, in_specs=[...  70.5 us

profile of v6, /device:TPU:0, one launch (start us, length us, event | category | flops | bytes accessed | tf_op | source)
XLA Modules:
  0.0 72.1 jit_solution(6645768060868834461)
XLA Ops:
  0.6 70.5 %shard_map.85 = (bf16[512,128]{1,0:T(8,128)(2,1)S(1)}, bf16[512,128]{1,0:T(8,128)(2,1)S(1)}, bf16[512,128]{1,0:T(8,128)(2,1)S(1)}) custom-call(bf16[512,128]{1,0:T(8,128)(2,1)} %bitcast.8, bf16[512,128]{1,0:T(8,128)(2,1)} %bitcast.9, bf16[512,128]{1,0:T(8,128)(2,1)} %bitcast.10, bf16[512,128]{1,0:T(8,128)(2,1)} %bitcast.11, bf16[512,128]{1,0:T(8,128)(2,1)} %bitcast.12, ...), custom_call_target="tpu_custom_call" | custom-call | tf_op jit(solution)/shard_map/pallas_call | solution.py:595
  71.2 0.8 %shard_map.86 = (bf16[512,128]{1,0:T(8,128)(2,1)}, bf16[512,128]{1,0:T(8,128)(2,1)}, bf16[512,128]{1,0:T(8,128)(2,1)}) custom-call(bf16[512,128]{1,0:T(8,128)(2,1)S(1)} %get-tuple-element.9.refs_0_, bf16[512,128]{1,0:T(8,128)(2,1)S(1)} %get-tuple-element.10.refs_1_, bf16[512,128]{1,0:T(8,128)(2,1)S(1)} %get-tuple-element.11.refs_2_), custom_call_target="tpu_custom_call" | custom-call | tf_op jit(solution)/shard_map/pallas_call | solution.py:602
